TPU v7x, 32 devices: a whole 2x2x4 slice. The times are simulated.
32 devices in a mesh: az: 8 (over z, y), rg: 4 (over x, core).
Axes of the slice: x: 2, y: 2, z: 4, core: 2. Of those that a mesh axis runs over, the one named last changes fastest.
Arguments:
- ref_image: float32 [1024, 3072], P('az', 'rg'), may hold values from 0.2 to 5
- sec_image: float32 [1024, 3072], P('az', 'rg'), may hold values from 0.2 to 5
- off_az: int32 [16], P('az'), may hold values from -7 to 7, as said below
- off_rg: int32 [16], P('az'), may hold values from -7 to 7, as said below
Outputs:
- surfaces: float32 [16, 48, 128, 128], P('az', 'rg')
Inputs may be any that keep to these rules, and one draw needn't show every extreme that they name: off_az is monotone over the chip rows, changes by 0 or 1 between neighbouring chip rows, and runs from one end of its range to the other. off_rg is monotone over the chip rows, changes by 0 or 1 between neighbouring chip rows, and runs from one end of its range to the other.
All inputs are finite; a program needn't handle non-finite values.
Results may differ from a plain program's by a relative error of at most 0.0003.
Values sent between devices are 32-bit elements; how exact they have to be, the bound alone decides.
No kernel may reach another device: no remote copies, remote signals or barrier semaphores. Data moves between devices by JAX's collectives and lax.ppermute only.
A program may use at most 64 MiB of HBM per device.

v0:
```python
import math

import jax
import jax.numpy as jnp
from jax import lax
from jax.sharding import PartitionSpec as P

CHIP = 128
SPACE = 64
SEARCH = 192
LAGS = 64


EPSILON = 1e-06
HIGH = lax.Precision.HIGH


def extended(value, sides, width):
    for axis, dim in sides:
        size, length = (lax.axis_size(axis), value.shape[dim])
        up = [(i, (i + 1) % size) for i in range(size - 1)]
        down = [(j, i) for i, j in up]
        last = lax.slice_in_dim(value, length - width, length, axis=dim)
        leading = lax.slice_in_dim(value, 0, width, axis=dim)
        before = lax.ppermute(last, axis, up)
        after = lax.ppermute(leading, axis, down)
        value = jnp.concatenate([before, value, after], axis=dim)
    return value


def box_matrix():
    lag_index = lax.iota(jnp.int32, LAGS)[:, None]
    cell_index = lax.iota(jnp.int32, SEARCH)[None, :]
    return ((cell_index >= lag_index) & (cell_index < lag_index + CHIP)).astype(jnp.float32)


def cubic_matrix():
    out_index = lax.iota(jnp.int32, 2 * LAGS)[:, None]
    sample = lax.iota(jnp.int32, LAGS)[None, :]
    base = out_index // 2

    def pick(where):
        return (jnp.clip(where, 0, LAGS - 1) == sample).astype(jnp.float32)

    even_part = pick(base)
    odd_part = (9.0 * (pick(base) + pick(base + 1)) - (pick(base - 1) + pick(base + 2))) / 16.0
    return jnp.where(out_index % 2 == 1, odd_part, even_part)


def fourier_tables():
    freq = lax.iota(jnp.int32, SEARCH)[:, None]
    cell = lax.iota(jnp.int32, SEARCH)[None, :]
    angle = (freq * cell % SEARCH).astype(jnp.float32) * (2.0 * math.pi / SEARCH)
    return (jnp.cos(angle), jnp.sin(angle))


def cut_chips(band, count):
    blocks = band.reshape(band.shape[0], count + 1, SPACE)
    joined = jnp.concatenate([blocks[:, :-1], blocks[:, 1:]], axis=2)
    return jnp.transpose(joined, (1, 0, 2))


def cut_windows(band, count):
    blocks = band.reshape(band.shape[0], count + 2, SPACE)
    joined = jnp.concatenate([blocks[:, :-2], blocks[:, 1:-1], blocks[:, 2:]], axis=2)
    return jnp.transpose(joined, (1, 0, 2))


def spectrum_of(field, left_cos, left_sin, right_cos, right_sin):
    first_re = jnp.einsum("ua,nab->nub", left_cos, field, precision=HIGH)
    first_im = -jnp.einsum("ua,nab->nub", left_sin, field, precision=HIGH)
    real_part = jnp.einsum("nub,vb->nuv", first_re, right_cos, precision=HIGH) + jnp.einsum(
        "nub,vb->nuv", first_im, right_sin, precision=HIGH
    )
    imag_part = jnp.einsum("nub,vb->nuv", first_im, right_cos, precision=HIGH) - jnp.einsum(
        "nub,vb->nuv", first_re, right_sin, precision=HIGH
    )
    return (real_part, imag_part)


def correlate(centered, windows):
    cosine, sine_table = fourier_tables()
    chip_re, chip_im = spectrum_of(
        centered, cosine[:, :CHIP], sine_table[:, :CHIP], cosine[:, :CHIP], sine_table[:, :CHIP]
    )
    win_re, win_im = spectrum_of(windows, cosine, sine_table, cosine, sine_table)
    prod_re = chip_re * win_re + chip_im * win_im
    prod_im = chip_re * win_im - chip_im * win_re
    back_cos = cosine[:LAGS]
    back_sin = sine_table[:LAGS]
    inner_re = jnp.einsum("pu,nuv->npv", back_cos, prod_re, precision=HIGH) - jnp.einsum(
        "pu,nuv->npv", back_sin, prod_im, precision=HIGH
    )
    inner_im = jnp.einsum("pu,nuv->npv", back_cos, prod_im, precision=HIGH) + jnp.einsum(
        "pu,nuv->npv", back_sin, prod_re, precision=HIGH
    )
    result = jnp.einsum("npv,qv->npq", inner_re, back_cos, precision=HIGH) - jnp.einsum(
        "npv,qv->npq", inner_im, back_sin, precision=HIGH
    )
    return result / float(SEARCH * SEARCH)


def finish(corr, centered, windows):
    box_sum = box_matrix()
    first = jnp.einsum("pr,nrs->nps", box_sum, windows, precision=HIGH)
    first = jnp.einsum("nps,qs->npq", first, box_sum, precision=HIGH)
    second = jnp.einsum("pr,nrs->nps", box_sum, windows * windows, precision=HIGH)
    second = jnp.einsum("nps,qs->npq", second, box_sum, precision=HIGH)
    area = float(CHIP * CHIP)
    var_sum = second - first * first / area
    energy = jnp.sum(centered * centered, axis=(1, 2))
    score = (
        CHIP * (corr / area) / jnp.sqrt(energy[:, None, None] / area * (var_sum / area) + EPSILON)
    )
    oversample = cubic_matrix()
    lifted = jnp.einsum("ap,npq->naq", oversample, score, precision=HIGH)
    return jnp.einsum("naq,bq->nab", lifted, oversample, precision=HIGH)


def body(ref_image, sec_image, off_az, off_rg):
    rows_dev = ref_image.shape[0]
    cols_dev = ref_image.shape[1]
    quarter = CHIP // 4
    half_chip = CHIP // 2
    chip_rows = rows_dev // SPACE
    chip_cols = cols_dev // SPACE
    all_rows = chip_rows * lax.axis_size("az")
    reach = min(half_chip - 1, (all_rows - 1) // 2)
    margin = half_chip + reach
    ref_ext = extended(ref_image, (("az", 0), ("rg", 1)), quarter)
    stacked = sec_image[None]
    widened = extended(extended(stacked, (("rg", 2),), margin), (("az", 1),), margin)
    sec_ext = widened[0]

    def one_row(inputs):
        row_index, shift_az, shift_rg = inputs
        ref_band = lax.dynamic_slice_in_dim(ref_ext, row_index * SPACE, CHIP, 0)
        chips = cut_chips(ref_band, chip_cols)
        sec_rows = lax.dynamic_slice_in_dim(
            sec_ext, row_index * SPACE + shift_az - half_chip + margin, SEARCH, 0
        )
        sec_band = lax.dynamic_slice_in_dim(
            sec_rows, shift_rg - half_chip + margin, chip_cols * SPACE + CHIP, 1
        )
        windows = cut_windows(sec_band, chip_cols)
        centered = chips - jnp.mean(chips, axis=(1, 2), keepdims=True)
        corr = correlate(centered, windows)
        return finish(corr, centered, windows)

    row_list = lax.iota(jnp.int32, chip_rows)
    return lax.map(one_row, (row_list, off_az, off_rg))


def solution(mesh):
    return jax.shard_map(
        body,
        mesh=mesh,
        in_specs=(P("az", "rg"), P("az", "rg"), P("az"), P("az")),
        out_specs=P("az", "rg", None, None),
        check_vma=False,
    )
```

profile of v0, /device:TPU:21, one launch (start us, length us, event | category | flops | bytes accessed | tf_op | source)
XLA Modules:
  0.0 149.6 jit_solution(13289463032613964204)
XLA Ops:
  0.0 1.1 copy.19
  1.2 3.7 %collective-permute-start.4 = (f32[1,128,71]{1,2,0:T(8,128)S(1)}, f32[1,128,71]{1,2,0:T(8,128)S(1)}, u32[]{:S(2)}, u32[]{:S(2)}) collective-permute-start(f32[1,128,71]{1,2,0:T(8,128)S(1)} %get-tuple-element.337), channel_id=1, source_target_pairs={{0,1},{1,2},{2,3},{4,5},{5,6},{6,7},{8,9},{9,10},{10,11},{12,13},{... | collective-permute-start | bytes 109064 | tf_op jit(solution)/shard_map/ppermute | solution.py:25
  4.9 1.9 %collective-permute-start.5 = (f32[1,128,71]{1,2,0:T(8,128)S(1)}, f32[1,128,71]{1,2,0:T(8,128)S(1)}, u32[]{:S(2)}, u32[]{:S(2)}) collective-permute-start(f32[1,128,71]{1,2,0:T(8,128)S(1)} %get-tuple-element.338), channel_id=1, source_target_pairs={{1,0},{2,1},{3,2},{5,4},{6,5},{7,6},{9,8},{10,9},{11,10},{13,12},{... | collective-permute-start | bytes 109064 | tf_op jit(solution)/shard_map/ppermute | solution.py:26
  6.8 1.2 copy.16
  8.1 3.1 %collective-permute-start = (f32[32,768]{0,1:T(8,128)S(1)}, f32[32,768]{0,1:T(8,128)S(1)}, u32[]{:S(2)}, u32[]{:S(2)}) collective-permute-start(f32[32,768]{0,1:T(8,128)S(1)} %get-tuple-element.339), channel_id=1, source_target_pairs={{0,4},{4,8},{8,12},{12,16},{16,20},{20,24},{24,28},{1,5},{5,9},{9,... | collective-permute-start | bytes 294920 | tf_op jit(solution)/shard_map/ppermute | solution.py:25
  11.3 2.1 %collective-permute-start.1 = (f32[32,768]{0,1:T(8,128)S(1)}, f32[32,768]{0,1:T(8,128)S(1)}, u32[]{:S(2)}, u32[]{:S(2)}) collective-permute-start(f32[32,768]{0,1:T(8,128)S(1)} %get-tuple-element.340), channel_id=1, source_target_pairs={{4,0},{8,4},{12,8},{16,12},{20,16},{24,20},{28,24},{5,1},{9,5},{13... | collective-permute-start | bytes 294920 | tf_op jit(solution)/shard_map/ppermute | solution.py:26
  13.5 1.0 fusion.122
  14.5 4.0 %collective-permute-start.6 = (f32[1,71,910]{1,2,0:T(8,128)}, f32[1,71,910]{1,2,0:T(8,128)}, u32[]{:S(2)}, u32[]{:S(2)}) collective-permute-start(f32[1,71,910]{1,2,0:T(8,128)} %get-tuple-element.335), channel_id=1, source_target_pairs={{0,4},{4,8},{8,12},{12,16},{16,20},{20,24},{24,28},{1,5},{5,9},{9,... | collective-permute-start | bytes 775328 | tf_op jit(solution)/shard_map/ppermute | solution.py:25
  18.5 1.9 %collective-permute-start.7 = (f32[1,71,910]{1,2,0:T(8,128)S(1)}, f32[1,71,910]{1,2,0:T(8,128)}, u32[]{:S(2)}, u32[]{:S(2)}) collective-permute-start(f32[1,71,910]{1,2,0:T(8,128)S(1)} %get-tuple-element.336), channel_id=1, source_target_pairs={{4,0},{8,4},{12,8},{16,12},{20,16},{24,20},{28,24},{5,1},{9,5},{13... | collective-permute-start | bytes 775328 | tf_op jit(solution)/shard_map/ppermute | solution.py:26
  20.4 19.3 %collective-permute-done = f32[32,768]{0,1:T(8,128)S(1)} collective-permute-done((f32[32,768]{0,1:T(8,128)S(1)}, f32[32,768]{0,1:T(8,128)S(1)}, u32[]{:S(2)}, u32[]{:S(2)}) %collective-permute-start) | collective-permute-done | bytes 98336 | tf_op jit(solution)/shard_map/ppermute | solution.py:25
  39.8 4.4 %collective-permute-start.2 = (f32[192,32]{0,1:T(8,128)S(1)}, f32[192,32]{0,1:T(8,128)S(1)}, u32[]{:S(2)}, u32[]{:S(2)}) collective-permute-start(f32[192,32]{0,1:T(8,128)S(1)} %get-tuple-element.333), channel_id=1, source_target_pairs={{0,1},{1,2},{2,3},{4,5},{5,6},{6,7},{8,9},{9,10},{10,11},{12,13},{... | collective-permute-start | bytes 73736 | tf_op jit(solution)/shard_map/ppermute | solution.py:25
  44.2 1.9 %collective-permute-start.3 = (f32[192,32]{0,1:T(8,128)S(1)}, f32[192,32]{0,1:T(8,128)S(1)}, u32[]{:S(2)}, u32[]{:S(2)}) collective-permute-start(f32[192,32]{0,1:T(8,128)S(1)} %get-tuple-element.334), channel_id=1, source_target_pairs={{1,0},{2,1},{3,2},{5,4},{6,5},{7,6},{9,8},{10,9},{11,10},{13,12},{... | collective-permute-start | bytes 73736 | tf_op jit(solution)/shard_map/ppermute | solution.py:26
  46.2 3.3 %collective-permute-done.3 = f32[192,32]{0,1:T(8,128)S(1)} collective-permute-done((f32[192,32]{0,1:T(8,128)S(1)}, f32[192,32]{0,1:T(8,128)S(1)}, u32[]{:S(2)}, u32[]{:S(2)}) %collective-permute-start.3) | collective-permute-done | bytes 24608 | tf_op jit(solution)/shard_map/ppermute | solution.py:26
  49.8 1.7 %maximum_bitcast_fusion.5 = f32[270,910]{0,1:T(8,128)S(1)} fusion(f32[1,71,910]{1,2,0:T(8,128)} %collective-permute-done.7, f32[1,128,71]{1,2,0:T(8,128)S(1)} %collective-permute-done.5, f32[1,128,768]{1,2,0:T(8,128)S(1)} %bitcast.245, f32[1,128,71]{1,2,0:T(8,128)S(1)} %collective-permute-done.4, f32[1,71,910]{1,2,0:T(8,128)} %collective-permute-done.6), kind=kLoop, calls=%fused_computation.147 | loop fusion | flops 982800 | bytes 1965600 | tf_op jit(solution)/shard_map/squeeze | solution.py:133
  51.6 97.0 %while.16 = (s32[]{:T(128)}, f32[2,12,128,128]{3,2,1,0:T(8,128)}, s32[2]{0:T(128)S(1)}, f32[192,832]{0,1:T(8,128)S(1)}, s32[2]{0:T(128)S(1)}, /*index=5*/s32[2]{...) while((s32[]{:T(128)}, f32[2,12,128,128]{3,2,1,0:T(8,128)}, ...), condition=%wide.region_4.5_spmd, body=%wide.region_0.4_spmd.sunk | while | flops 6243618816 | bytes 102016920 | solution.py:151
  56.2 0.8 fusion.238
  57.0 0.8 fusion.236
  58.7 0.7 fusion.239
  60.4 0.8 fusion.230
  61.3 0.8 convolution_bitcast_fusion.7
  62.1 0.8 fusion.229
  62.9 0.8 fusion.231
  63.8 1.9 %fusion.234 = f32[12,192,192]{2,1,0:T(8,128)S(1)} fusion(f32[192,12,64]{0,2,1:T(8,128)S(1)} %get-tuple-element.397, f32[192,12,64]{0,2,1:T(8,128)S(1)} %get-tuple-element.398, f32[192,12,64]{0,2,1:T(8,128)S(1)} %get-tuple-element.399), kind=kOutput, calls=%fused_computation.47.clone.1 | convolution fusion | flops 510824448 | bytes 3538944 | tf_op jit(solution)/shard_map/while/body/eval_jaxpr/ua,nab->nub/dot_general | solution.py:70
  65.6 1.9 %fusion.232 = f32[12,192,192]{2,1,0:T(8,128)S(1)} fusion(f32[192,12,64]{0,2,1:T(8,128)S(1)} %get-tuple-element.397, f32[192,12,64]{0,2,1:T(8,128)S(1)} %get-tuple-element.398, f32[192,12,64]{0,2,1:T(8,128)S(1)} %get-tuple-element.399), kind=kOutput, calls=%fused_computation.46.clone.1 | convolution fusion | flops 510824448 | bytes 3538944 | tf_op jit(solution)/shard_map/while/body/eval_jaxpr/ua,nab->nub/dot_general | solution.py:71
  67.5 3.6 %fusion.240 = f32[12,192,192]{2,1,0:T(8,128)S(1)} fusion(f32[12,192,192]{2,1,0:T(8,128)S(1)} %fusion.232), kind=kOutput, calls=%fused_computation.1.clone.1 | convolution fusion | flops 510382080 | bytes 3538944 | tf_op jit(solution)/shard_map/while/body/eval_jaxpr/nub,vb->nuv/dot_general | solution.py:75
  71.1 3.0 %fusion.233 = f32[12,192,192]{2,1,0:T(8,128)S(1)} fusion(f32[12,192,192]{2,1,0:T(8,128)S(1)} %fusion.232), kind=kOutput, calls=%fused_computation.3.clone.1 | convolution fusion | flops 510382080 | bytes 3538944 | tf_op jit(solution)/shard_map/while/body/eval_jaxpr/nub,vb->nuv/dot_general | solution.py:72
  74.1 3.0 %fusion.235 = f32[12,192,192]{2,1,0:T(8,128)S(1)} fusion(f32[12,192,192]{2,1,0:T(8,128)S(1)} %fusion.233, f32[12,192,192]{2,1,0:T(8,128)S(1)} %fusion.234), kind=kOutput, calls=%fused_computation.17.clone.1 | convolution fusion | flops 510382080 | bytes 5308416 | tf_op jit(solution)/shard_map/while/body/eval_jaxpr/nub,vb->nuv/dot_general | solution.py:72
  77.2 3.0 %fusion.241 = f32[12,192,192]{2,1,0:T(8,128)S(1)} fusion(f32[12,192,192]{2,1,0:T(8,128)S(1)} %fusion.240, f32[12,192,192]{2,1,0:T(8,128)S(1)} %fusion.234), kind=kOutput, calls=%fused_computation.18.clone.1 | convolution fusion | flops 510382080 | bytes 5308416 | tf_op jit(solution)/shard_map/while/body/eval_jaxpr/nub,vb->nuv/dot_general | solution.py:75
  80.2 1.1 fusion.237
  81.3 1.3 convolution_add_fusion.3
  82.7 1.1 fusion.242
  83.8 1.5 %multiply_subtract_fusion.2 = (f32[12,192,192]{2,1,0:T(8,128)S(1)}, f32[12,192,192]{2,1,0:T(8,128)S(1)}) fusion(f32[12,192,192]{2,1,0:T(8,128)S(1)} %fusion.235, f32[12,192,192]{2,1,0:T(8,128)S(1)} %convolution_add_fusion.3, f32[12,192,192]{2,1,0:T(8,128)S(1)} %fusion.241, f32[12,192,192]{2,1,0:T(8,128)S(1)} %fusion.242, ...), kind=kOutput, calls=%fused_computation.11.clone.1 | convolution fusion | flops 342835200 | bytes 14254080 | tf_op jit(solution)/shard_map/while/body/eval_jaxpr/nub,vb->nuv/dot_general | solution.py:75
  85.3 2.4 %fusion.243 = f32[12,192,64]{2,1,0:T(8,128)S(1)} fusion(f32[12,192,192]{2,1,0:T(8,128)S(1)} %get-tuple-element.404, f32[192,192]{1,0:T(8,128)S(1)} %fusion.236), kind=kOutput, calls=%fused_computation.78.clone.1 | convolution fusion | flops 169869312 | bytes 3014656 | tf_op jit(solution)/shard_map/while/body/eval_jaxpr/pu,nuv->npv/dot_general | solution.py:91
  87.7 2.4 %fusion.244 = f32[12,64,192]{1,2,0:T(8,128)S(1)} fusion(f32[12,192,64]{2,1,0:T(8,128)S(1)} %fusion.243, f32[12,192,192]{2,1,0:T(8,128)S(1)} %get-tuple-element.405, f32[192,192]{1,0:T(8,128)S(1)} %fusion.238), kind=kOutput, calls=%fused_computation.22.clone.1 | convolution fusion | flops 170016768 | bytes 4194304 | tf_op jit(solution)/shard_map/while/body/eval_jaxpr/pu,nuv->npv/dot_general | solution.py:91
  90.1 2.4 %fusion.246 = f32[12,192,64]{2,1,0:T(8,128)S(1)} fusion(f32[12,192,192]{2,1,0:T(8,128)S(1)} %get-tuple-element.405, f32[192,192]{1,0:T(8,128)S(1)} %fusion.236), kind=kOutput, calls=%fused_computation.76.clone.1 | convolution fusion | flops 169869312 | bytes 3014656 | tf_op jit(solution)/shard_map/while/body/eval_jaxpr/pu,nuv->npv/dot_general | solution.py:94
  92.5 2.4 %fusion.247 = f32[12,64,192]{1,2,0:T(8,128)S(1)} fusion(f32[12,192,64]{2,1,0:T(8,128)S(1)} %fusion.246, f32[12,192,192]{2,1,0:T(8,128)S(1)} %get-tuple-element.404, f32[192,192]{1,0:T(8,128)S(1)} %fusion.238), kind=kOutput, calls=%fused_computation.20.clone.1 | convolution fusion | flops 170016768 | bytes 4194304 | tf_op jit(solution)/shard_map/while/body/eval_jaxpr/pu,nuv->npv/dot_general | solution.py:94
  94.9 1.2 fusion.245
  96.1 1.2 fusion.248
  97.7 0.8 fusion.250
  98.6 1.1 copy-done.1
  104.5 0.8 fusion.238
  105.2 0.8 fusion.236
  108.6 0.8 fusion.230
  109.5 0.8 convolution_bitcast_fusion.7
  110.4 0.8 fusion.229
  111.2 0.8 fusion.231
  112.0 1.8 %fusion.234 = f32[12,192,192]{2,1,0:T(8,128)S(1)} fusion(f32[192,12,64]{0,2,1:T(8,128)S(1)} %get-tuple-element.397, f32[192,12,64]{0,2,1:T(8,128)S(1)} %get-tuple-element.398, f32[192,12,64]{0,2,1:T(8,128)S(1)} %get-tuple-element.399), kind=kOutput, calls=%fused_computation.47.clone.1 | convolution fusion | flops 510824448 | bytes 3538944 | tf_op jit(solution)/shard_map/while/body/eval_jaxpr/ua,nab->nub/dot_general | solution.py:70
  113.9 1.9 %fusion.232 = f32[12,192,192]{2,1,0:T(8,128)S(1)} fusion(f32[192,12,64]{0,2,1:T(8,128)S(1)} %get-tuple-element.397, f32[192,12,64]{0,2,1:T(8,128)S(1)} %get-tuple-element.398, f32[192,12,64]{0,2,1:T(8,128)S(1)} %get-tuple-element.399), kind=kOutput, calls=%fused_computation.46.clone.1 | convolution fusion | flops 510824448 | bytes 3538944 | tf_op jit(solution)/shard_map/while/body/eval_jaxpr/ua,nab->nub/dot_general | solution.py:71
  115.8 3.2 %fusion.240 = f32[12,192,192]{2,1,0:T(8,128)S(1)} fusion(f32[12,192,192]{2,1,0:T(8,128)S(1)} %fusion.232), kind=kOutput, calls=%fused_computation.1.clone.1 | convolution fusion | flops 510382080 | bytes 3538944 | tf_op jit(solution)/shard_map/while/body/eval_jaxpr/nub,vb->nuv/dot_general | solution.py:75
  118.9 3.0 %fusion.233 = f32[12,192,192]{2,1,0:T(8,128)S(1)} fusion(f32[12,192,192]{2,1,0:T(8,128)S(1)} %fusion.232), kind=kOutput, calls=%fused_computation.3.clone.1 | convolution fusion | flops 510382080 | bytes 3538944 | tf_op jit(solution)/shard_map/while/body/eval_jaxpr/nub,vb->nuv/dot_general | solution.py:72
  122.0 3.0 %fusion.235 = f32[12,192,192]{2,1,0:T(8,128)S(1)} fusion(f32[12,192,192]{2,1,0:T(8,128)S(1)} %fusion.233, f32[12,192,192]{2,1,0:T(8,128)S(1)} %fusion.234), kind=kOutput, calls=%fused_computation.17.clone.1 | convolution fusion | flops 510382080 | bytes 5308416 | tf_op jit(solution)/shard_map/while/body/eval_jaxpr/nub,vb->nuv/dot_general | solution.py:72
  125.0 3.0 %fusion.241 = f32[12,192,192]{2,1,0:T(8,128)S(1)} fusion(f32[12,192,192]{2,1,0:T(8,128)S(1)} %fusion.240, f32[12,192,192]{2,1,0:T(8,128)S(1)} %fusion.234), kind=kOutput, calls=%fused_computation.18.clone.1 | convolution fusion | flops 510382080 | bytes 5308416 | tf_op jit(solution)/shard_map/while/body/eval_jaxpr/nub,vb->nuv/dot_general | solution.py:75
  128.0 1.1 fusion.237
  129.2 1.6 %convolution_add_fusion.3 = f32[12,192,192]{2,1,0:T(8,128)S(1)} fusion(f32[12,192,192]{2,1,0:T(8,128)S(1)} %fusion.237, f32[12,192,128]{2,1,0:T(8,128)S(1)} %fusion.239, f32[192,192]{1,0:T(8,128)S(1)} %fusion.238), kind=kOutput, calls=%fused_computation.16.clone.1 | convolution fusion | flops 340180992 | bytes 5406720 | tf_op jit(solution)/shard_map/while/body/eval_jaxpr/nub,vb->nuv/dot_general | solution.py:72
  130.7 1.1 fusion.242
  131.8 1.5 multiply_subtract_fusion.2
  133.3 2.4 %fusion.243 = f32[12,192,64]{2,1,0:T(8,128)S(1)} fusion(f32[12,192,192]{2,1,0:T(8,128)S(1)} %get-tuple-element.404, f32[192,192]{1,0:T(8,128)S(1)} %fusion.236), kind=kOutput, calls=%fused_computation.78.clone.1 | convolution fusion | flops 169869312 | bytes 3014656 | tf_op jit(solution)/shard_map/while/body/eval_jaxpr/pu,nuv->npv/dot_general | solution.py:91
  135.7 2.4 %fusion.244 = f32[12,64,192]{1,2,0:T(8,128)S(1)} fusion(f32[12,192,64]{2,1,0:T(8,128)S(1)} %fusion.243, f32[12,192,192]{2,1,0:T(8,128)S(1)} %get-tuple-element.405, f32[192,192]{1,0:T(8,128)S(1)} %fusion.238), kind=kOutput, calls=%fused_computation.22.clone.1 | convolution fusion | flops 170016768 | bytes 4194304 | tf_op jit(solution)/shard_map/while/body/eval_jaxpr/pu,nuv->npv/dot_general | solution.py:91
  138.2 2.4 %fusion.246 = f32[12,192,64]{2,1,0:T(8,128)S(1)} fusion(f32[12,192,192]{2,1,0:T(8,128)S(1)} %get-tuple-element.405, f32[192,192]{1,0:T(8,128)S(1)} %fusion.236), kind=kOutput, calls=%fused_computation.76.clone.1 | convolution fusion | flops 169869312 | bytes 3014656 | tf_op jit(solution)/shard_map/while/body/eval_jaxpr/pu,nuv->npv/dot_general | solution.py:94
  140.5 2.4 %fusion.247 = f32[12,64,192]{1,2,0:T(8,128)S(1)} fusion(f32[12,192,64]{2,1,0:T(8,128)S(1)} %fusion.246, f32[12,192,192]{2,1,0:T(8,128)S(1)} %get-tuple-element.404, f32[192,192]{1,0:T(8,128)S(1)} %fusion.238), kind=kOutput, calls=%fused_computation.20.clone.1 | convolution fusion | flops 170016768 | bytes 4194304 | tf_op jit(solution)/shard_map/while/body/eval_jaxpr/pu,nuv->npv/dot_general | solution.py:94
  143.0 1.2 fusion.245
  144.1 1.2 fusion.248
  145.8 0.8 fusion.250
  146.6 1.1 copy-done.1
  (56 shorter events, 10.0 us)
Async XLA Ops:
  1.2 12.3 %collective-permute-start.4 = (f32[1,128,71]{1,2,0:T(8,128)S(1)}, f32[1,128,71]{1,2,0:T(8,128)S(1)}, u32[]{:S(2)}, u32[]{:S(2)}) collective-permute-start(f32[1,128,71]{1,2,0:T(8,128)S(1)} %get-tuple-element.337), channel_id=1, source_target_pairs={{0,1},{1,2},{2,3},{4,5},{5,6},{6,7},{8,9},{9,10},{10,11},{12,13},{... | collective-permute-start | bytes 109064 | tf_op jit(solution)/shard_map/ppermute | solution.py:25
  4.9 8.6 %collective-permute-start.5 = (f32[1,128,71]{1,2,0:T(8,128)S(1)}, f32[1,128,71]{1,2,0:T(8,128)S(1)}, u32[]{:S(2)}, u32[]{:S(2)}) collective-permute-start(f32[1,128,71]{1,2,0:T(8,128)S(1)} %get-tuple-element.338), channel_id=1, source_target_pairs={{1,0},{2,1},{3,2},{5,4},{6,5},{7,6},{9,8},{10,9},{11,10},{13,12},{... | collective-permute-start | bytes 109064 | tf_op jit(solution)/shard_map/ppermute | solution.py:26
  8.1 31.6 %collective-permute-start = (f32[32,768]{0,1:T(8,128)S(1)}, f32[32,768]{0,1:T(8,128)S(1)}, u32[]{:S(2)}, u32[]{:S(2)}) collective-permute-start(f32[32,768]{0,1:T(8,128)S(1)} %get-tuple-element.339), channel_id=1, source_target_pairs={{0,4},{4,8},{8,12},{12,16},{16,20},{20,24},{24,28},{1,5},{5,9},{9,... | collective-permute-start | bytes 294920 | tf_op jit(solution)/shard_map/ppermute | solution.py:25
  11.3 28.4 %collective-permute-start.1 = (f32[32,768]{0,1:T(8,128)S(1)}, f32[32,768]{0,1:T(8,128)S(1)}, u32[]{:S(2)}, u32[]{:S(2)}) collective-permute-start(f32[32,768]{0,1:T(8,128)S(1)} %get-tuple-element.340), channel_id=1, source_target_pairs={{4,0},{8,4},{12,8},{16,12},{20,16},{24,20},{28,24},{5,1},{9,5},{13... | collective-permute-start | bytes 294920 | tf_op jit(solution)/shard_map/ppermute | solution.py:26
  14.5 35.3 %collective-permute-start.6 = (f32[1,71,910]{1,2,0:T(8,128)}, f32[1,71,910]{1,2,0:T(8,128)}, u32[]{:S(2)}, u32[]{:S(2)}) collective-permute-start(f32[1,71,910]{1,2,0:T(8,128)} %get-tuple-element.335), channel_id=1, source_target_pairs={{0,4},{4,8},{8,12},{12,16},{16,20},{20,24},{24,28},{1,5},{5,9},{9,... | collective-permute-start | bytes 775328 | tf_op jit(solution)/shard_map/ppermute | solution.py:25
  18.5 31.3 %collective-permute-start.7 = (f32[1,71,910]{1,2,0:T(8,128)S(1)}, f32[1,71,910]{1,2,0:T(8,128)}, u32[]{:S(2)}, u32[]{:S(2)}) collective-permute-start(f32[1,71,910]{1,2,0:T(8,128)S(1)} %get-tuple-element.336), channel_id=1, source_target_pairs={{4,0},{8,4},{12,8},{16,12},{20,16},{24,20},{28,24},{5,1},{9,5},{13... | collective-permute-start | bytes 775328 | tf_op jit(solution)/shard_map/ppermute | solution.py:26
  39.8 6.4 %collective-permute-start.2 = (f32[192,32]{0,1:T(8,128)S(1)}, f32[192,32]{0,1:T(8,128)S(1)}, u32[]{:S(2)}, u32[]{:S(2)}) collective-permute-start(f32[192,32]{0,1:T(8,128)S(1)} %get-tuple-element.333), channel_id=1, source_target_pairs={{0,1},{1,2},{2,3},{4,5},{5,6},{6,7},{8,9},{9,10},{10,11},{12,13},{... | collective-permute-start | bytes 73736 | tf_op jit(solution)/shard_map/ppermute | solution.py:25
  44.2 5.2 %collective-permute-start.3 = (f32[192,32]{0,1:T(8,128)S(1)}, f32[192,32]{0,1:T(8,128)S(1)}, u32[]{:S(2)}, u32[]{:S(2)}) collective-permute-start(f32[192,32]{0,1:T(8,128)S(1)} %get-tuple-element.334), channel_id=1, source_target_pairs={{1,0},{2,1},{3,2},{5,4},{6,5},{7,6},{9,8},{10,9},{11,10},{13,12},{... | collective-permute-start | bytes 73736 | tf_op jit(solution)/shard_map/ppermute | solution.py:26
  46.1 5.4 %copy-start.2 = (s32[2]{0:T(128)S(1)}, s32[2]{0:T(128)}, u32[]{:S(2)}) copy-start(s32[2]{0:T(128)} %param.8) | copy-start | bytes 28
  46.2 5.4 %copy-start.3 = (s32[2]{0:T(128)S(1)}, s32[2]{0:T(128)}, u32[]{:S(2)}) copy-start(s32[2]{0:T(128)} %param.9) | copy-start | bytes 28
  94.9 2.8 %copy-start = (f32[2,12,128,128]{3,2,1,0:T(8,128)S(1)}, f32[2,12,128,128]{3,2,1,0:T(8,128)}, u32[]{:S(2)}) copy-start(f32[2,12,128,128]{3,2,1,0:T(8,128)} %get-tuple-element.428) | copy-start | bytes 4718596 | tf_op jit(solution)/shard_map/while
  98.5 1.1 copy-start.1
  143.0 2.8 %copy-start = (f32[2,12,128,128]{3,2,1,0:T(8,128)S(1)}, f32[2,12,128,128]{3,2,1,0:T(8,128)}, u32[]{:S(2)}) copy-start(f32[2,12,128,128]{3,2,1,0:T(8,128)} %get-tuple-element.428) | copy-start | bytes 4718596 | tf_op jit(solution)/shard_map/while
  146.6 1.1 copy-start.1
where the time goes:
time: 152 us; the launch traced here: 150 us
  matrix products  78.6 us (52%)
  starting transfers between devices  23.2 us (15%)
  waiting for transfers between devices  22.5 us (15%)
  local copies, waits for them, and re-layouts  11 us (7%)
  loops' own time  6.88 us (5%)
  other arithmetic  6.23 us (4%)
    ppermute x4, waiting for transfers between devices, extended(): before = lax.ppermute(last, axis, up)  19.3 us
    ppermute x4, starting transfers between devices, extended(): before = lax.ppermute(last, axis, up)  15.3 us
    dot_general x4, matrix products, spectrum_of(): jnp.einsum('nub,vb->nuv', first_re, right_sin, precision=HIGH)  9.04 us
    dot_general x4, matrix products, spectrum_of(): jnp.einsum('nub,vb->nuv', first_im, right_cos, precision=HIGH)  9.01 us
    dot_general x4, matrix products, spectrum_of(): jnp.einsum('nub,vb->nuv', first_im, right_sin, precision=HIGH)  8.93 us
    dot_general x4, matrix products, spectrum_of(): jnp.einsum('nub,vb->nuv', first_re, right_cos, precision=HIGH)  8.27 us
    ppermute x4, starting transfers between devices, extended(): after = lax.ppermute(leading, axis, down)  7.9 us
    another operation x1, loops' own time, body(): return lax.map(one_row, (row_list, off_az, off_rg))  6.88 us
  transfers between devices with their start and end apart: 8, of which 2 were waited for; matrix products, arithmetic and copies ran while one was open for 2% of the time, Pallas kernels for 0%

commit v1 on v0

v1 whole, which is shorter than its diff:
```python
import functools
import math

import jax
import jax.numpy as jnp
import numpy as np
from jax import lax
from jax.experimental import pallas as pl
from jax.experimental.pallas import tpu as pltpu
from jax.sharding import PartitionSpec as P

CHIP = 128
SPACE = 64
SEARCH = 192
LAGS = 64
LANES = 128
FREQ = SEARCH // 2
EPSILON = 1e-06
AREA = float(CHIP * CHIP)
BF16 = jnp.bfloat16
F32 = jnp.float32


def halves(table):
    high = table.astype(BF16)
    low = (table - high.astype(np.float64)).astype(BF16)
    return high, low


@functools.cache
def tables():
    theta = 2.0 * math.pi * (np.arange(FREQ)[:, None] + 0.5) / SEARCH
    cell = np.arange(SEARCH)[None, :]
    forward = np.concatenate([np.cos(theta * cell), -np.sin(theta * cell)], axis=0)
    lag = np.arange(LAGS)[:, None]
    box = ((cell >= lag) & (cell < lag + CHIP)).astype(np.float64)
    high, low = halves(np.concatenate([forward, box], axis=0))
    rows_sec = np.concatenate([high, high, low], axis=1)
    high, low = halves(forward[:, :CHIP])
    rows_ref = np.concatenate([high, high, low], axis=1)
    rows_box = np.concatenate([box, box], axis=1).astype(BF16)

    phi = 2.0 * math.pi / CHIP * np.arange(CHIP)[None, :]
    spot = np.arange(SPACE)[:, None]
    cosine, sine = np.cos(phi * spot), np.sin(phi * spot)
    block = np.concatenate(
        [np.concatenate([cosine, -sine], axis=1), np.concatenate([sine, cosine], axis=1)], axis=0
    )
    spread = np.zeros((4 * SPACE, 4 * CHIP))
    for half in range(2):
        for part in range(2):
            spread[2 * SPACE * part + SPACE * half:][:SPACE, 2 * CHIP * half:][:, : 2 * CHIP] = block[
                SPACE * part:][:SPACE]
    high, low = halves(spread)
    columns = np.concatenate([high, high, low], axis=0)

    back = np.zeros((4 * CHIP, 4 * LAGS))
    cosine, sine = np.cos(phi.T * lag.T), np.sin(phi.T * lag.T)
    for half in range(2):
        base = 2 * CHIP * half
        back[base:base + CHIP, LAGS * half:LAGS * (half + 1)] = cosine
        back[base:base + CHIP, LAGS * (2 + half):LAGS * (3 + half)] = sine
        back[base + CHIP:base + 2 * CHIP, LAGS * half:LAGS * (half + 1)] = -sine
        back[base + CHIP:base + 2 * CHIP, LAGS * (2 + half):LAGS * (3 + half)] = cosine
    high, low = halves(back)
    back_columns = np.concatenate([high, high, low], axis=0)

    final = np.concatenate([np.cos(theta.T * lag), -np.sin(theta.T * lag)], axis=1)
    high, low = halves(final * (2.0 / (SEARCH * CHIP)))
    back_rows = np.concatenate([high, high, low], axis=1)

    wide = np.arange(2 * LANES)[:, None]
    lane = np.arange(LANES)[None, :]
    slide = ((wide >= lane) & (wide < lane + CHIP)).astype(np.float64)
    start = lane // SPACE * SPACE
    gather = ((wide >= start) & (wide < start + CHIP)).astype(np.float64)
    slide = np.concatenate([slide, slide], axis=0).astype(BF16)
    gather = np.concatenate([gather, gather, gather], axis=0).astype(BF16)

    out_index = np.arange(2 * LAGS)[:, None]
    sample = np.arange(LAGS)[None, :]
    base = out_index // 2

    def pick(where):
        return (np.clip(where, 0, LAGS - 1) == sample).astype(np.float64)

    odd = (9.0 * (pick(base) + pick(base + 1)) - (pick(base - 1) + pick(base + 2))) / 16.0
    cubic = np.where(out_index % 2 == 1, odd, pick(base))
    cubic_rows = np.concatenate([cubic, cubic], axis=1).astype(BF16)
    zero = np.zeros_like(cubic.T)
    pair = np.concatenate(
        [np.concatenate([cubic.T, zero], axis=1), np.concatenate([zero, cubic.T], axis=1)], axis=0
    )
    cubic_cols = np.concatenate([pair, pair], axis=0).astype(BF16)
    return (rows_sec, rows_ref, rows_box, columns, back_columns, back_rows, slide, gather,
            cubic_rows, cubic_cols)


def split(value):
    high = value.astype(BF16)
    low = (value - high.astype(F32)).astype(BF16)
    return high, low


def dot(left, right):
    return jnp.dot(left, right, preferred_element_type=F32)


def pack_kernel(pad, side, sec_l, sec_r, ref_l, ref_r, up_l, up_r, down_l, down_r, right_out, left_out):
    rows = sec_l.shape[0]
    lane = lax.broadcasted_iota(jnp.int32, (1, LANES), 1)

    def tile(out, up, sec, down, ref, shift, keep):
        out[0:pad] = up[0:pad]
        out[pad:pad + rows] = sec[...]
        out[pad + rows:pad + rows + pad] = down[0:pad]
        inner = jnp.concatenate([up[pad:pad + side], ref[...], down[pad:pad + side]], axis=0)
        here = slice(pad - side, pad + rows + side)
        out[here] = jnp.where(keep, out[here], pltpu.roll(inner, shift, 1))

    tile(right_out, up_r, sec_r, down_r, ref_r, side, lane >= side)
    tile(left_out, up_l, sec_l, down_l, ref_l, LANES - side, lane < LANES - side)


def main_kernel(pad, side, off_az, off_rg, sec, ref, up, down, left, right, rows_sec, rows_ref, rows_box,
                columns, back_columns, back_rows, slide, gather, cubic_rows, cubic_cols, out,
                sec_ext, ref_ext, lhs, spec, zed):
    rows, cols = sec.shape
    tiles = cols // LANES
    step = pl.program_id(0)
    width = cols + 2 * LANES
    band = cols + LANES

    @pl.when(step == 0)
    def _():
        level_sec = jnp.sum(sec[...]) * (1.0 / (rows * cols))
        level_ref = jnp.sum(ref[...]) * (1.0 / (rows * cols))
        inner = slice(LANES, LANES + cols)
        sec_ext[0:pad, inner] = up[0:pad] - level_sec
        sec_ext[pad:pad + rows, inner] = sec[...] - level_sec
        sec_ext[pad + rows:, inner] = down[0:pad] - level_sec
        sec_ext[:, 0:LANES] = left[...] - level_sec
        sec_ext[:, LANES + cols:] = right[...] - level_sec
        here = slice(pad - side, pad + rows + side)
        middle = jnp.concatenate([up[pad:pad + side], ref[...], down[pad:pad + side]], axis=0)
        whole = jnp.concatenate(
            [pltpu.roll(left[here], LANES - side, 1), middle, pltpu.roll(right[here], side, 1)], axis=1)
        ref_ext[...] = pltpu.roll(whole, width - (LANES - side), 1)[:, :band] - level_ref

    start = step * SPACE + (pad - SPACE) + off_az[step]
    aligned = pl.multiple_of(start // 8 * 8, 8)
    field = sec_ext[pl.ds(aligned, SEARCH + 8), :]
    field = pltpu.roll(field, width - SPACE - off_rg[step], 1)[:, :band]
    field = pltpu.roll(field, SEARCH + 8 - (start - aligned), 0)[:SEARCH]
    high, low = split(field)
    spectrum = dot(rows_sec[...], jnp.concatenate([high, low, high], axis=0))
    square_high, square_low = split(field * field)
    second = dot(rows_box[...], jnp.concatenate([square_high, square_low], axis=0))
    first = spectrum[2 * FREQ:]
    chips = ref_ext[pl.ds(pl.multiple_of(step * SPACE, SPACE), CHIP), :]
    high, low = split(chips)
    chip_spectrum = dot(rows_ref[...], jnp.concatenate([high, low, high], axis=0))
    count = tiles + 1
    for which, source in enumerate((spectrum, chip_spectrum)):
        for t in range(count):
            here = slice(t * LANES, (t + 1) * LANES)
            both = jnp.concatenate([source[:FREQ, here], source[FREQ:2 * FREQ, here]], axis=1)
            high, low = split(both)
            row = (which * count + t) * FREQ
            lhs[row:row + FREQ, :] = jnp.concatenate([high, low], axis=1)
    both = lhs[...]
    spec[...] = dot(jnp.concatenate([both, both[:, :2 * LANES]], axis=1), columns[...])

    sign = (1 - 2 * (lax.broadcasted_iota(jnp.int32, (1, LANES), 1) % 2)).astype(F32)

    def block(which, b):
        row = (which * count + b // 2) * FREQ
        base = 2 * CHIP * (b % 2)
        return spec[row:row + FREQ, base:base + CHIP], spec[row:row + FREQ, base + CHIP:base + 2 * CHIP]

    def product(b):
        (w_re, w_im), (n_re, n_im), (c_re, c_im) = block(0, b), block(0, b + 1), block(1, b)
        p_re, p_im = w_re + sign * n_re, w_im + sign * n_im
        return c_re * p_re + c_im * p_im, c_re * p_im - c_im * p_re

    chips_here = 2 * tiles
    before = product(0)
    for c in range(chips_here):
        after = product(c + 1)
        both = jnp.concatenate([before[0] + after[0], before[1] + after[1]], axis=1)
        high, low = split(both)
        row, base = (c // 2) * FREQ, 2 * CHIP * (c % 2)
        zed[row:row + FREQ, base:base + 2 * CHIP] = high
        zed[row:row + FREQ, 4 * CHIP + base:4 * CHIP + base + 2 * CHIP] = low
        before = after
    both = zed[...]
    lags = dot(jnp.concatenate([both, both[:, :4 * CHIP]], axis=1), back_columns[...])
    pieces = [lags[t * FREQ:(t + 1) * FREQ] for t in range(tiles)]
    stacked = jnp.concatenate(
        [jnp.concatenate([piece[:, :LANES], piece[:, LANES:]], axis=0) for piece in pieces], axis=1)
    high, low = split(stacked)
    raw = dot(back_rows[...], jnp.concatenate([high, low, high], axis=0))

    sums = jnp.concatenate([first, second], axis=0)
    sums = jnp.concatenate([sums[:, t * LANES:(t + 2) * LANES] for t in range(tiles)], axis=0)
    high, low = split(sums)
    boxes = dot(jnp.concatenate([high, low], axis=1), slide[...])
    totals = jnp.concatenate(
        [jnp.sum(chips.reshape(CHIP // 8, 8, band), axis=0),
         jnp.sum((chips * chips).reshape(CHIP // 8, 8, band), axis=0)], axis=0)
    totals = jnp.concatenate([totals[:, t * LANES:(t + 2) * LANES] for t in range(tiles)], axis=0)
    high, low = split(totals)
    rest = (totals - high.astype(F32) - low.astype(F32)).astype(BF16)
    totals = dot(jnp.concatenate([high, low, rest], axis=1), gather[...])

    scores = []
    for t in range(tiles):
        first_t = boxes[t * CHIP:t * CHIP + LAGS]
        second_t = boxes[t * CHIP + LAGS:(t + 1) * CHIP]
        total = jnp.sum(totals[16 * t:16 * t + 8], axis=0, keepdims=True)
        power = jnp.sum(totals[16 * t + 8:16 * t + 16], axis=0, keepdims=True)
        corr = raw[:, t * LANES:(t + 1) * LANES] - (total * (1.0 / AREA)) * first_t
        var_sum = second_t - first_t * first_t * (1.0 / AREA)
        energy = power - total * total * (1.0 / AREA)
        scores.append(CHIP * (corr * (1.0 / AREA)) * lax.rsqrt(
            (energy * (1.0 / AREA)) * (var_sum * (1.0 / AREA)) + EPSILON))
    high, low = split(jnp.concatenate(scores, axis=1))
    lifted = dot(cubic_rows[...], jnp.concatenate([high, low], axis=0))
    lifted = jnp.concatenate([lifted[:, t * LANES:(t + 1) * LANES] for t in range(tiles)], axis=0)
    high, low = split(lifted)
    fine = dot(jnp.concatenate([high, low], axis=1), cubic_cols[...])
    for c in range(chips_here):
        row, base = (c // 2) * CHIP, CHIP * (c % 2)
        out[0, c] = fine[row:row + CHIP, base:base + CHIP]


def neighbours(axis):
    size = lax.axis_size(axis)
    forth = [(i, i + 1) for i in range(size - 1)]
    return forth, [(j, i) for i, j in forth]


def body(ref_image, sec_image, off_az, off_rg):
    rows, cols = ref_image.shape
    side = CHIP // 4
    chip_rows, chip_cols = rows // SPACE, cols // SPACE
    all_rows = chip_rows * lax.axis_size("az")
    reach = min(SPACE - 1, (all_rows - 1) // 2)
    pad = -(-(SPACE + reach) // 8) * 8
    assert SPACE + reach + side <= LANES
    tiles = cols // LANES

    forth, back = neighbours("az")
    up = lax.ppermute(jnp.concatenate([sec_image[rows - pad:], ref_image[rows - side:]], axis=0), "az", forth)
    down = lax.ppermute(jnp.concatenate([sec_image[:pad], ref_image[:side]], axis=0), "az", back)

    tall = rows + 2 * pad

    def end(index, height):
        return pl.BlockSpec((height, LANES), lambda i, index=index: (0, index))

    ends = [end(i, h) for h in (rows, rows, pad + side, pad + side) for i in (0, tiles - 1)]
    to_right, to_left = pl.pallas_call(
        functools.partial(pack_kernel, pad, side),
        grid=(1,),
        in_specs=ends,
        out_specs=[pl.BlockSpec((tall, LANES), lambda i: (0, 0))] * 2,
        out_shape=[jax.ShapeDtypeStruct((tall, LANES), F32)] * 2,
    )(sec_image, sec_image, ref_image, ref_image, up, up, down, down)
    forth, back = neighbours("rg")
    left = lax.ppermute(to_right, "rg", forth)
    right = lax.ppermute(to_left, "rg", back)

    constants = [jnp.asarray(t) for t in tables()]
    operands = [sec_image, ref_image, up, down, left, right, *constants]
    count = tiles + 1

    def whole(x):
        return pl.BlockSpec(x.shape, lambda i, *_: (0, 0), pipeline_mode=pl.Buffered(1))

    return pl.pallas_call(
        functools.partial(main_kernel, pad, side),
        grid_spec=pltpu.PrefetchScalarGridSpec(
            num_scalar_prefetch=2,
            grid=(chip_rows,),
            in_specs=[whole(x) for x in operands],
            out_specs=pl.BlockSpec((1, chip_cols, 2 * LAGS, 2 * LAGS), lambda i, *_: (i, 0, 0, 0)),
            scratch_shapes=[
                pltpu.VMEM((tall, cols + 2 * LANES), F32),
                pltpu.VMEM((rows + 2 * side, cols + LANES), F32),
                pltpu.VMEM((2 * count * FREQ, 4 * LANES), BF16),
                pltpu.VMEM((2 * count * FREQ, 4 * CHIP), F32),
                pltpu.VMEM((tiles * FREQ, 8 * CHIP), BF16),
            ],
        ),
        out_shape=jax.ShapeDtypeStruct((chip_rows, chip_cols, 2 * LAGS, 2 * LAGS), F32),
        compiler_params=pltpu.CompilerParams(dimension_semantics=("arbitrary",), vmem_limit_bytes=48 << 20),
    )(off_az, off_rg, *operands)


def solution(mesh):
    return jax.shard_map(
        body,
        mesh=mesh,
        in_specs=(P("az", "rg"), P("az", "rg"), P("az"), P("az")),
        out_specs=P("az", "rg", None, None),
        check_vma=False,
    )
```

time: 152 us -> 53.7 us (0.35); the launches traced: 150 us -> 52.9 us
  matrix products: 78.6 us -> 0 us
  Pallas kernels: 0 us -> 13.4 us
  starting transfers between devices: 23.2 us -> 12 us
  loops' own time: 6.88 us -> 0 us
  waiting for transfers between devices: 22.5 us -> 16.1 us
  other arithmetic: 6.23 us -> 0.05 us
    dot_general x48 -> x0, matrix products: 78.6 us -> none  [the longest x4 9.04 us: spectrum_of(): jnp.einsum('nub,vb->nuv', first_re, right_sin, precision=HIGH)]
    pallas_call x0 -> x2, Pallas kernels: none -> 13.4 us  [the longest x1 11.6 us: body(): pl.pallas_call(functools.partial(main_kernel, pad, side), grid_spec=pltpu...]
    ppermute x8 -> x4, starting transfers between devices: 23.2 us -> 12 us  [the longest x1 4.52 us: body(): left = lax.ppermute(to_right, 'rg', forth)]
    another operation x1 -> x0, loops' own time: 6.88 us -> none  [body(): return lax.map(one_row, (row_list, off_az, off_rg))]
    unnamed x6 -> x36, local copies, waits for them, and re-layouts: 2.32 us -> 9.12 us
    ppermute x8 -> x4, waiting for transfers between devices: 22.5 us -> 16.1 us  [the longest x1 11.5 us: body(): lax.ppermute(jnp.concatenate([sec_image[rows - pad:], ref_image[rows - si...]
    dynamic_slice x10 -> x0, local copies, waits for them, and re-layouts: 4.65 us -> none  [the longest x6 3.67 us: body(): return lax.map(one_row, (row_list, off_az, off_rg))]
    while x8 -> x0, local copies, waits for them, and re-layouts: 2.29 us -> none
  transfers between devices with their start and end apart: 8 -> 4, of which waited for: 2 -> 3; matrix products, arithmetic and copies ran while one was open for 2% -> 0% of each run, Pallas kernels for 0% -> 0%
where the time goes in v1:
time: 53.7 us; the launch traced here: 52.9 us
  waiting for transfers between devices  16.1 us (30%)
  Pallas kernels  13.4 us (25%)
  starting transfers between devices  12 us (22%)
  local copies, waits for them, and re-layouts  11.2 us (21%)
    pallas_call x1, Pallas kernels, body(): pl.pallas_call(functools.partial(main_kernel, pad, side), grid_spec=pltpu...  11.6 us
    ppermute x1, waiting for transfers between devices, body(): lax.ppermute(jnp.concatenate([sec_image[rows - pad:], ref_image[rows - si...  11.5 us
    unnamed x36, local copies, waits for them, and re-layouts  9.12 us
    ppermute x1, starting transfers between devices, body(): left = lax.ppermute(to_right, 'rg', forth)  4.52 us
    ppermute x1, waiting for transfers between devices, body(): right = lax.ppermute(to_left, 'rg', back)  4.27 us
    ppermute x1, starting transfers between devices, body(): lax.ppermute(jnp.concatenate([sec_image[rows - pad:], ref_image[rows - si...  3.15 us
    ppermute x1, starting transfers between devices, body(): lax.ppermute(jnp.concatenate([sec_image[:pad], ref_image[:side]], axis=0)...  2.4 us
    ppermute x1, starting transfers between devices, body(): right = lax.ppermute(to_left, 'rg', back)  1.92 us
  transfers between devices with their start and end apart: 4, of which 3 were waited for; matrix products, arithmetic and copies ran while one was open for 0% of the time, Pallas kernels for 0%

profile of v1, /device:TPU:21, one launch (start us, length us, event | category | flops | bytes accessed | tf_op | source)
XLA Modules:
  0.0 52.9 jit_solution(11327289105132133072)
XLA Ops:
  0.0 1.0 %fusion.1 = (f32[32,768]{1,0:T(8,128)S(1)}, f32[32,768]{1,0:T(8,128)S(1)}) fusion(f32[128,768]{1,0:T(8,128)} %ref.1), kind=kLoop, calls=%fused_computation.3 | loop fusion | bytes 393216 | tf_op jit(solution)/shard_map/slice | solution.py:255
  1.0 1.1 %fusion = (f32[72,768]{1,0:T(8,128)S(1)}, f32[72,768]{1,0:T(8,128)S(1)}) fusion(f32[128,768]{1,0:T(8,128)} %sec.1), kind=kLoop, calls=%fused_computation.2 | loop fusion | bytes 884736 | tf_op jit(solution)/shard_map/slice | solution.py:255
  2.1 3.1 %collective-permute-start = (f32[104,768]{1,0:T(8,128)S(1)}, f32[104,768]{1,0:T(8,128)S(1)}, u32[]{:S(2)}, u32[]{:S(2)}) collective-permute-start(f32[104,768]{1,0:T(8,128)S(1)} %pad_maximum_fusion), channel_id=1, source_target_pairs={{0,4},{4,8},{8,12},{12,16},{16,20},{20,24},{24,28},{1,5},{5,9},{9,... | collective-permute-start | bytes 958472 | tf_op jit(solution)/shard_map/ppermute | solution.py:254
  5.2 0.0 copy-start.9
  5.3 0.0 copy-start
  5.3 0.0 copy-start.1
  5.3 0.0 copy-start.6
  5.3 0.0 copy-start.7
  5.3 0.0 copy-start.8
  5.3 0.0 copy-start.15
  5.3 2.4 %collective-permute-start.1 = (f32[104,768]{1,0:T(8,128)S(1)}, f32[104,768]{1,0:T(8,128)S(1)}, u32[]{:S(2)}, u32[]{:S(2)}) collective-permute-start(f32[104,768]{1,0:T(8,128)S(1)} %pad_maximum_fusion.1), channel_id=1, source_target_pairs={{4,0},{8,4},{12,8},{16,12},{20,16},{24,20},{28,24},{5,1},{9,5},{13... | collective-permute-start | bytes 958472 | tf_op jit(solution)/shard_map/ppermute | solution.py:255
  7.7 11.5 %collective-permute-done.up_l.up_r.up = f32[104,768]{1,0:T(8,128)S(1)} collective-permute-done((f32[104,768]{1,0:T(8,128)S(1)}, f32[104,768]{1,0:T(8,128)S(1)}, u32[]{:S(2)}, u32[]{:S(2)}) %collective-permute-start) | collective-permute-done | bytes 319520 | tf_op jit(solution)/shard_map/ppermute | solution.py:254
  19.2 0.0 copy-start.2
  19.2 0.0 collective-permute-done.1.down_l.down_r.down
  19.2 0.7 %copy-done.2 = f32[104,768]{1,0:T(8,128)} copy-done((f32[104,768]{1,0:T(8,128)}, f32[104,768]{1,0:T(8,128)S(1)}, u32[]{:S(2)}) %copy-start.2) | copy-done | bytes 319512
  19.9 0.0 copy-start.4
  20.0 0.7 %copy-done.4 = f32[104,768]{1,0:T(8,128)} copy-done((f32[104,768]{1,0:T(8,128)}, f32[104,768]{1,0:T(8,128)S(1)}, u32[]{:S(2)}) %copy-start.4) | copy-done | bytes 319512
  20.7 1.8 %shard_map.136 = (f32[272,128]{1,0:T(8,128)}, f32[272,128]{1,0:T(8,128)}) custom-call(f32[128,768]{1,0:T(8,128)} %sec.1, f32[128,768]{1,0:T(8,128)} %sec.1, f32[128,768]{1,0:T(8,128)} %ref.1, f32[128,768]{1,0:T(8,128)} %ref.1, f32[104,768]{1,0:T(8,128)} %copy-done.2, f32[104,768]{1,0:T(8,128)} %copy-done.2, f32[104,768]{1,0:T(8,128)} %copy-done.4, ...), custom_call_target="tpu_custom_call" | custom-call | tf_op jit(solution)/shard_map/pallas_call | solution.py:263
  22.5 4.5 %collective-permute-start.2 = (f32[272,128]{1,0:T(8,128)}, f32[272,128]{1,0:T(8,128)S(1)}, u32[]{:S(2)}, u32[]{:S(2)}) collective-permute-start(f32[272,128]{1,0:T(8,128)} %get-tuple-element.7), channel_id=1, source_target_pairs={{0,1},{1,2},{2,3},{4,5},{5,6},{6,7},{8,9},{9,10},{10,11},{12,13},{... | collective-permute-start | bytes 417800 | tf_op jit(solution)/shard_map/ppermute | solution.py:271
  27.0 1.9 %collective-permute-start.3 = (f32[272,128]{1,0:T(8,128)}, f32[272,128]{1,0:T(8,128)S(1)}, u32[]{:S(2)}, u32[]{:S(2)}) collective-permute-start(f32[272,128]{1,0:T(8,128)} %get-tuple-element.8), channel_id=1, source_target_pairs={{1,0},{2,1},{3,2},{5,4},{6,5},{7,6},{9,8},{10,9},{11,10},{13,12},{... | collective-permute-start | bytes 417800 | tf_op jit(solution)/shard_map/ppermute | solution.py:272
  28.9 0.4 collective-permute-done.2.left
  29.3 4.3 %collective-permute-done.3.right = f32[272,128]{1,0:T(8,128)S(1)} collective-permute-done((f32[272,128]{1,0:T(8,128)}, f32[272,128]{1,0:T(8,128)S(1)}, u32[]{:S(2)}, u32[]{:S(2)}) %collective-permute-start.3) | collective-permute-done | bytes 139296 | tf_op jit(solution)/shard_map/ppermute | solution.py:272
  33.6 0.0 copy-done.9
  33.6 0.0 copy-done
  33.6 0.0 copy-done.1
  33.6 0.0 copy-done.6
  33.6 0.0 copy-done.7
  33.6 0.0 copy-done.8
  33.6 0.0 copy-done.15
  33.6 0.0 copy-start.3
  33.7 1.0 %copy-done.3 = f32[104,768]{1,0:T(8,128)S(1)} copy-done((f32[104,768]{1,0:T(8,128)S(1)}, f32[104,768]{1,0:T(8,128)}, u32[]{:S(2)}) %copy-start.3) | copy-done | bytes 319512
  34.6 0.0 copy-start.5
  34.6 1.0 %copy-done.5 = f32[104,768]{1,0:T(8,128)S(1)} copy-done((f32[104,768]{1,0:T(8,128)S(1)}, f32[104,768]{1,0:T(8,128)}, u32[]{:S(2)}) %copy-start.5) | copy-done | bytes 319512
  35.6 0.0 copy-start.10
  35.6 0.9 %copy-done.10 = bf16[192,384]{1,0:T(8,128)(2,1)S(1)} copy-done((bf16[192,384]{1,0:T(8,128)(2,1)S(1)}, bf16[192,384]{1,0:T(8,128)(2,1)}, u32[]{:S(2)}) %copy-start.10) | copy-done | bytes 147480
  36.5 0.0 copy-start.11
  36.5 0.9 %copy-done.11 = bf16[256,256]{1,0:T(8,128)(2,1)S(1)} copy-done((bf16[256,256]{1,0:T(8,128)(2,1)S(1)}, bf16[256,256]{1,0:T(8,128)(2,1)}, u32[]{:S(2)}) %copy-start.11) | copy-done | bytes 131096
  37.4 0.0 copy-start.12
  37.4 0.9 %copy-done.12 = bf16[512,128]{1,0:T(8,128)(2,1)S(1)} copy-done((bf16[512,128]{1,0:T(8,128)(2,1)S(1)}, bf16[512,128]{1,0:T(8,128)(2,1)}, u32[]{:S(2)}) %copy-start.12) | copy-done | bytes 131096
  38.3 0.0 copy-start.13
  38.3 0.9 %copy-done.13 = bf16[64,576]{1,0:T(8,128)(2,1)S(1)} copy-done((bf16[64,576]{1,0:T(8,128)(2,1)S(1)}, bf16[64,576]{1,0:T(8,128)(2,1)}, u32[]{:S(2)}) %copy-start.13) | copy-done | bytes 73752
  39.2 0.0 copy-start.14
  39.2 0.8 %copy-done.14 = bf16[64,384]{1,0:T(8,128)(2,1)S(1)} copy-done((bf16[64,384]{1,0:T(8,128)(2,1)S(1)}, bf16[64,384]{1,0:T(8,128)(2,1)}, u32[]{:S(2)}) %copy-start.14) | copy-done | bytes 49176
  40.0 0.0 copy-start.16
  40.0 0.7 %copy-done.16 = s32[2]{0:T(128)S(1)} copy-done((s32[2]{0:T(128)S(1)}, s32[2]{0:T(128)}, u32[]{:S(2)}) %copy-start.16) | copy-done | bytes 32
  40.7 0.0 copy-start.17
  40.7 0.7 %copy-done.17 = s32[2]{0:T(128)S(1)} copy-done((s32[2]{0:T(128)S(1)}, s32[2]{0:T(128)}, u32[]{:S(2)}) %copy-start.17) | copy-done | bytes 32
  41.3 11.6 %shard_map.137 = f32[2,12,128,128]{3,2,1,0:T(8,128)} custom-call(s32[2]{0:T(128)S(1)} %copy-done.16, s32[2]{0:T(128)S(1)} %copy-done.17, f32[128,768]{1,0:T(8,128)S(1)} %copy-done, f32[128,768]{1,0:T(8,128)S(1)} %copy-done.1, f32[104,768]{1,0:T(8,128)S(1)} %copy-done.3, f32[104,768]{1,0:T(8,128)S(1)} %copy-done.5, ...), custom_call_target="tpu_custom_call" | custom-call | tf_op jit(solution)/shard_map/pallas_call | solution.py:281
  (2 shorter events, 0.0 us)
Async XLA Ops:
  2.1 17.2 %collective-permute-start = (f32[104,768]{1,0:T(8,128)S(1)}, f32[104,768]{1,0:T(8,128)S(1)}, u32[]{:S(2)}, u32[]{:S(2)}) collective-permute-start(f32[104,768]{1,0:T(8,128)S(1)} %pad_maximum_fusion), channel_id=1, source_target_pairs={{0,4},{4,8},{8,12},{12,16},{16,20},{20,24},{24,28},{1,5},{5,9},{9,... | collective-permute-start | bytes 958472 | tf_op jit(solution)/shard_map/ppermute | solution.py:254
  5.2 28.4 %copy-start.9 = (bf16[768,128]{1,0:T(8,128)(2,1)S(1)}, bf16[768,128]{1,0:T(8,128)(2,1)}, u32[]{:S(2)}) copy-start(bf16[768,128]{1,0:T(8,128)(2,1)} %constant.27.clone.gather) | copy-start | bytes 589828
  5.3 28.3 %copy-start = (f32[128,768]{1,0:T(8,128)S(1)}, f32[128,768]{1,0:T(8,128)}, u32[]{:S(2)}) copy-start(f32[128,768]{1,0:T(8,128)} %sec.1) | copy-start | bytes 1179652
  5.3 28.3 %copy-start.1 = (f32[128,768]{1,0:T(8,128)S(1)}, f32[128,768]{1,0:T(8,128)}, u32[]{:S(2)}) copy-start(f32[128,768]{1,0:T(8,128)} %ref.1) | copy-start | bytes 1179652
  5.3 28.3 %copy-start.6 = (bf16[1536,256]{1,0:T(8,128)(2,1)S(1)}, bf16[1536,256]{1,0:T(8,128)(2,1)}, u32[]{:S(2)}) copy-start(bf16[1536,256]{1,0:T(8,128)(2,1)} %constant.24.clone.back_columns) | copy-start | bytes 2359300
  5.3 28.3 %copy-start.7 = (bf16[768,512]{1,0:T(8,128)(2,1)S(1)}, bf16[768,512]{1,0:T(8,128)(2,1)}, u32[]{:S(2)}) copy-start(bf16[768,512]{1,0:T(8,128)(2,1)} %constant.23.clone.columns) | copy-start | bytes 2359300
  5.3 28.3 %copy-start.8 = (bf16[256,576]{1,0:T(8,128)(2,1)S(1)}, bf16[256,576]{1,0:T(8,128)(2,1)}, u32[]{:S(2)}) copy-start(bf16[256,576]{1,0:T(8,128)(2,1)} %constant.20.clone.rows_sec) | copy-start | bytes 884740
  5.3 28.3 %copy-start.15 = (bf16[128,128]{1,0:T(8,128)(2,1)S(1)}, bf16[128,128]{1,0:T(8,128)(2,1)}, u32[]{:S(2)}) copy-start(bf16[128,128]{1,0:T(8,128)(2,1)} %constant.28.clone.cubic_rows) | copy-start | bytes 98308
  5.3 13.9 %collective-permute-start.1 = (f32[104,768]{1,0:T(8,128)S(1)}, f32[104,768]{1,0:T(8,128)S(1)}, u32[]{:S(2)}, u32[]{:S(2)}) collective-permute-start(f32[104,768]{1,0:T(8,128)S(1)} %pad_maximum_fusion.1), channel_id=1, source_target_pairs={{4,0},{8,4},{12,8},{16,12},{20,16},{24,20},{28,24},{5,1},{9,5},{13... | collective-permute-start | bytes 958472 | tf_op jit(solution)/shard_map/ppermute | solution.py:255
  19.2 0.7 %copy-start.2 = (f32[104,768]{1,0:T(8,128)}, f32[104,768]{1,0:T(8,128)S(1)}, u32[]{:S(2)}) copy-start(f32[104,768]{1,0:T(8,128)S(1)} %collective-permute-done.up_l.up_r.up) | copy-start | bytes 958468
  19.9 0.7 %copy-start.4 = (f32[104,768]{1,0:T(8,128)}, f32[104,768]{1,0:T(8,128)S(1)}, u32[]{:S(2)}) copy-start(f32[104,768]{1,0:T(8,128)S(1)} %collective-permute-done.1.down_l.down_r.down) | copy-start | bytes 958468
  22.5 6.8 %collective-permute-start.2 = (f32[272,128]{1,0:T(8,128)}, f32[272,128]{1,0:T(8,128)S(1)}, u32[]{:S(2)}, u32[]{:S(2)}) collective-permute-start(f32[272,128]{1,0:T(8,128)} %get-tuple-element.7), channel_id=1, source_target_pairs={{0,1},{1,2},{2,3},{4,5},{5,6},{6,7},{8,9},{9,10},{10,11},{12,13},{... | collective-permute-start | bytes 417800 | tf_op jit(solution)/shard_map/ppermute | solution.py:271
  27.0 6.6 %collective-permute-start.3 = (f32[272,128]{1,0:T(8,128)}, f32[272,128]{1,0:T(8,128)S(1)}, u32[]{:S(2)}, u32[]{:S(2)}) collective-permute-start(f32[272,128]{1,0:T(8,128)} %get-tuple-element.8), channel_id=1, source_target_pairs={{1,0},{2,1},{3,2},{5,4},{6,5},{7,6},{9,8},{10,9},{11,10},{13,12},{... | collective-permute-start | bytes 417800 | tf_op jit(solution)/shard_map/ppermute | solution.py:272
  33.6 1.0 %copy-start.3 = (f32[104,768]{1,0:T(8,128)S(1)}, f32[104,768]{1,0:T(8,128)}, u32[]{:S(2)}) copy-start(f32[104,768]{1,0:T(8,128)} %copy-done.2) | copy-start | bytes 958468
  34.6 1.0 %copy-start.5 = (f32[104,768]{1,0:T(8,128)S(1)}, f32[104,768]{1,0:T(8,128)}, u32[]{:S(2)}) copy-start(f32[104,768]{1,0:T(8,128)} %copy-done.4) | copy-start | bytes 958468
  35.6 0.9 %copy-start.10 = (bf16[192,384]{1,0:T(8,128)(2,1)S(1)}, bf16[192,384]{1,0:T(8,128)(2,1)}, u32[]{:S(2)}) copy-start(bf16[192,384]{1,0:T(8,128)(2,1)} %constant.21.clone.rows_ref) | copy-start | bytes 442372
  36.5 0.9 %copy-start.11 = (bf16[256,256]{1,0:T(8,128)(2,1)S(1)}, bf16[256,256]{1,0:T(8,128)(2,1)}, u32[]{:S(2)}) copy-start(bf16[256,256]{1,0:T(8,128)(2,1)} %constant.29.clone.cubic_cols) | copy-start | bytes 393220
  37.4 0.9 %copy-start.12 = (bf16[512,128]{1,0:T(8,128)(2,1)S(1)}, bf16[512,128]{1,0:T(8,128)(2,1)}, u32[]{:S(2)}) copy-start(bf16[512,128]{1,0:T(8,128)(2,1)} %constant.26.clone.slide) | copy-start | bytes 393220
  38.3 0.9 %copy-start.13 = (bf16[64,576]{1,0:T(8,128)(2,1)S(1)}, bf16[64,576]{1,0:T(8,128)(2,1)}, u32[]{:S(2)}) copy-start(bf16[64,576]{1,0:T(8,128)(2,1)} %constant.25.clone.back_rows) | copy-start | bytes 221188
  39.2 0.8 %copy-start.14 = (bf16[64,384]{1,0:T(8,128)(2,1)S(1)}, bf16[64,384]{1,0:T(8,128)(2,1)}, u32[]{:S(2)}) copy-start(bf16[64,384]{1,0:T(8,128)(2,1)} %constant.22.clone.rows_box) | copy-start | bytes 147460
  40.0 0.7 %copy-start.16 = (s32[2]{0:T(128)S(1)}, s32[2]{0:T(128)}, u32[]{:S(2)}) copy-start(s32[2]{0:T(128)} %off_az.1) | copy-start | bytes 28
  40.7 0.7 %copy-start.17 = (s32[2]{0:T(128)S(1)}, s32[2]{0:T(128)}, u32[]{:S(2)}) copy-start(s32[2]{0:T(128)} %off_rg.1) | copy-start | bytes 28

commit v2 on v1

v2 whole, which is shorter than its diff:
```python
import functools
import math

import jax
import jax.numpy as jnp
import numpy as np
from jax import lax
from jax.experimental import pallas as pl
from jax.experimental.pallas import tpu as pltpu
from jax.sharding import PartitionSpec as P

CHIP = 128
SPACE = 64
SEARCH = 192
LAGS = 64
LANES = 128
FREQ = SEARCH // 2
EPSILON = 1e-06
AREA = float(CHIP * CHIP)
BF16 = jnp.bfloat16
F32 = jnp.float32


def halves(table):
    high = table.astype(BF16)
    low = (table - high.astype(np.float64)).astype(BF16)
    return high, low


@functools.cache
def tables():
    theta = 2.0 * math.pi * (np.arange(FREQ)[:, None] + 0.5) / SEARCH
    cell = np.arange(SEARCH)[None, :]
    forward = np.concatenate([np.cos(theta * cell), -np.sin(theta * cell)], axis=0)
    lag = np.arange(LAGS)[:, None]
    box = ((cell >= lag) & (cell < lag + CHIP)).astype(np.float64)
    made = {}
    high, low = halves(np.concatenate([forward, box], axis=0))
    made["rows_sec"] = np.concatenate([high, high, low], axis=1)
    high, low = halves(forward[:, :CHIP])
    made["rows_ref"] = np.concatenate([high, high, low], axis=1)
    made["rows_box"] = np.concatenate([box, box], axis=1).astype(BF16)

    phi = 2.0 * math.pi / CHIP * np.arange(CHIP)[None, :]
    spot = np.arange(SPACE)[:, None]
    cosine, sine = np.cos(phi * spot), np.sin(phi * spot)
    parts = (np.concatenate([cosine, -sine], axis=1), np.concatenate([sine, cosine], axis=1))
    spread = np.zeros((4 * SPACE, 4 * CHIP))
    for half in range(2):
        for part in range(2):
            row = 2 * SPACE * part + SPACE * half
            spread[row:row + SPACE, 2 * CHIP * half:2 * CHIP * (half + 1)] = parts[part]
    made["columns"] = np.concatenate(halves(spread), axis=0)

    back = np.zeros((4 * CHIP, 4 * LAGS))
    cosine, sine = np.cos(phi.T * lag.T), np.sin(phi.T * lag.T)
    for half in range(2):
        base = 2 * CHIP * half
        back[base:base + CHIP, LAGS * half:LAGS * (half + 1)] = cosine
        back[base:base + CHIP, LAGS * (2 + half):LAGS * (3 + half)] = sine
        back[base + CHIP:base + 2 * CHIP, LAGS * half:LAGS * (half + 1)] = -sine
        back[base + CHIP:base + 2 * CHIP, LAGS * (2 + half):LAGS * (3 + half)] = cosine
    made["back_columns"] = np.concatenate(halves(back), axis=0)

    final = np.concatenate([np.cos(theta.T * lag), -np.sin(theta.T * lag)], axis=1)
    high, low = halves(final * (2.0 / (SEARCH * CHIP)))
    made["back_rows"] = np.concatenate([high, high, low], axis=1)

    wide = np.arange(2 * LANES)[:, None]
    lane = np.arange(LANES)[None, :]
    start = lane // SPACE * SPACE
    made["slide"] = ((wide >= lane) & (wide < lane + CHIP)).astype(BF16)
    made["gather"] = ((wide >= start) & (wide < start + CHIP)).astype(BF16)

    out_index = np.arange(2 * LAGS)[:, None]
    sample = np.arange(LAGS)[None, :]
    base = out_index // 2

    def pick(where):
        return (np.clip(where, 0, LAGS - 1) == sample).astype(np.float64)

    odd = (9.0 * (pick(base) + pick(base + 1)) - (pick(base - 1) + pick(base + 2))) / 16.0
    cubic = np.where(out_index % 2 == 1, odd, pick(base))
    made["cubic_rows"] = np.concatenate([cubic, cubic], axis=1).astype(BF16)
    zero = np.zeros_like(cubic.T)
    made["cubic_cols"] = np.concatenate(
        [np.concatenate([cubic.T, zero], axis=1), np.concatenate([zero, cubic.T], axis=1)], axis=0
    ).astype(BF16)

    slabs, places, top = [], {}, 0
    for name, table in made.items():
        table = np.pad(table, ((0, 0), (0, -table.shape[1] % LANES)))
        pieces = [table[:, i:i + LANES] for i in range(0, table.shape[1], LANES)]
        places[name] = (top, table.shape[0], len(pieces), made[name].shape[1])
        slabs += pieces
        top += table.shape[0] * len(pieces)
    return np.concatenate(slabs, axis=0), places


def split(value):
    high = value.astype(BF16)
    low = (value - high.astype(F32)).astype(BF16)
    return high, low


def dot(left, right):
    return jnp.dot(left, right, preferred_element_type=F32)


def pack_kernel(pad, side, sec_hbm, ref_hbm, sec, ref, up, down, right, left, sems):
    rows, cols = sec.shape
    copies = [
        pltpu.make_async_copy(source, target, sems.at[i])
        for i, (source, target) in enumerate([
            (sec_hbm, sec),
            (ref_hbm, ref),
            (sec_hbm.at[pl.ds(rows - pad, pad)], up.at[pl.ds(0, pad)]),
            (sec_hbm.at[pl.ds(0, pad)], down.at[pl.ds(0, pad)]),
            (ref_hbm.at[pl.ds(rows - side, side)], up.at[pl.ds(pad, side)]),
            (ref_hbm.at[pl.ds(0, side)], down.at[pl.ds(pad, side)]),
        ])
    ]
    for copy in copies:
        copy.start()
    copies[0].wait()
    copies[1].wait()
    lane = lax.broadcasted_iota(jnp.int32, (1, LANES), 1)
    right[...] = jnp.where(lane >= side, sec[:, cols - LANES:], pltpu.roll(ref[:, cols - LANES:], side, 1))
    left[...] = jnp.where(lane < LANES - side, sec[:, :LANES], pltpu.roll(ref[:, :LANES], LANES - side, 1))
    for copy in copies[2:]:
        copy.wait()


def corner_kernel(pad, left, right, up, down):
    rows = left.shape[0]
    up[:, :LANES] = left[rows - pad:]
    up[:, LANES:] = right[rows - pad:]
    down[:, :LANES] = left[:pad]
    down[:, LANES:] = right[:pad]


def main_kernel(pad, side, off_az_hbm, off_rg_hbm, slab_hbm, sec, ref, up, down, left, right, corner_up,
                corner_down, out, slab, off_az, off_rg, sec_ext, ref_ext, lhs, spec, zed, sems):
    rows, cols = sec.shape
    tiles = cols // LANES
    step = pl.program_id(0)
    width = cols + 2 * LANES
    band = cols + LANES

    def table(name):
        top, height, count, last = tables()[1][name]
        pieces = [slab[top + i * height:top + (i + 1) * height, :] for i in range(count)]
        value = jnp.concatenate(pieces, axis=1) if count > 1 else pieces[0]
        return value[:, :last]

    def twice(name):
        value = table(name)
        half = value.shape[0] // 2
        return jnp.concatenate([value[:half], value], axis=0)

    @pl.when(step == 0)
    def _():
        copies = [
            pltpu.make_async_copy(source, target, sems.at[i])
            for i, (source, target) in enumerate(
                [(slab_hbm, slab), (off_az_hbm, off_az), (off_rg_hbm, off_rg)])
        ]
        for copy in copies:
            copy.start()
        level_sec = jnp.sum(sec[...]) * (1.0 / (rows * cols))
        level_ref = jnp.sum(ref[...]) * (1.0 / (rows * cols))
        inner = slice(LANES, LANES + cols)
        sec_ext[0:pad, 0:LANES] = corner_up[:, :LANES] - level_sec
        sec_ext[0:pad, inner] = up[0:pad] - level_sec
        sec_ext[0:pad, LANES + cols:] = corner_up[:, LANES:] - level_sec
        sec_ext[pad:pad + rows, 0:LANES] = left[...] - level_sec
        sec_ext[pad:pad + rows, inner] = sec[...] - level_sec
        sec_ext[pad:pad + rows, LANES + cols:] = right[...] - level_sec
        sec_ext[pad + rows:, 0:LANES] = corner_down[:, :LANES] - level_sec
        sec_ext[pad + rows:, inner] = down[0:pad] - level_sec
        sec_ext[pad + rows:, LANES + cols:] = corner_down[:, LANES:] - level_sec
        lane = lax.broadcasted_iota(jnp.int32, (1, LANES), 1)

        def place(at, west, middle, east):
            pieces = [pltpu.roll(west, LANES - side, 1)]
            pieces += [middle[:, t * LANES:(t + 1) * LANES] for t in range(tiles)]
            pieces += [pltpu.roll(east, side, 1)]
            turned = [pltpu.roll(piece, side, 1) for piece in pieces]
            for t in range(tiles + 1):
                ref_ext[at:at + west.shape[0], t * LANES:(t + 1) * LANES] = jnp.where(
                    lane < side, turned[t], turned[t + 1]) - level_ref

        place(0, corner_up[pad - side:, :LANES], up[pad:], corner_up[pad - side:, LANES:])
        place(side, left[...], ref[...], right[...])
        place(side + rows, corner_down[:side, :LANES], down[pad:], corner_down[:side, LANES:])
        for copy in copies:
            copy.wait()

    start = step * SPACE + (pad - SPACE) + off_az[step]
    aligned = pl.multiple_of(start // 8 * 8, 8)
    field = sec_ext[pl.ds(aligned, SEARCH + 8), :]
    shift = LANES - SPACE - off_rg[step]
    turned = [pltpu.roll(field[:, t * LANES:(t + 1) * LANES], shift, 1) for t in range(tiles + 2)]
    lane = lax.broadcasted_iota(jnp.int32, (1, LANES), 1)
    field = jnp.concatenate(
        [jnp.where(lane < shift, turned[t], turned[t + 1]) for t in range(tiles + 1)], axis=1)
    field = pltpu.roll(field, SEARCH + 8 - (start - aligned), 0)[:SEARCH]
    high, low = split(field)
    spectrum = dot(table("rows_sec"), jnp.concatenate([high, low, high], axis=0))
    square_high, square_low = split(field * field)
    second = dot(table("rows_box"), jnp.concatenate([square_high, square_low], axis=0))
    first = spectrum[2 * FREQ:]
    chips = ref_ext[pl.ds(pl.multiple_of(step * SPACE, SPACE), CHIP), :]
    high, low = split(chips)
    chip_spectrum = dot(table("rows_ref"), jnp.concatenate([high, low, high], axis=0))
    count = tiles + 1
    for which, source in enumerate((spectrum, chip_spectrum)):
        for t in range(count):
            here = slice(t * LANES, (t + 1) * LANES)
            both = jnp.concatenate([source[:FREQ, here], source[FREQ:2 * FREQ, here]], axis=1)
            high, low = split(both)
            row = (which * count + t) * FREQ
            lhs[row:row + FREQ, :] = jnp.concatenate([high, low], axis=1)
    both = lhs[...]
    spec[...] = dot(jnp.concatenate([both, both[:, :2 * LANES]], axis=1), twice("columns"))

    sign = (1 - 2 * (lax.broadcasted_iota(jnp.int32, (1, LANES), 1) % 2)).astype(F32)

    def block(which, b):
        row = (which * count + b // 2) * FREQ
        base = 2 * CHIP * (b % 2)
        return spec[row:row + FREQ, base:base + CHIP], spec[row:row + FREQ, base + CHIP:base + 2 * CHIP]

    def product(b):
        (w_re, w_im), (n_re, n_im), (c_re, c_im) = block(0, b), block(0, b + 1), block(1, b)
        p_re, p_im = w_re + sign * n_re, w_im + sign * n_im
        return c_re * p_re + c_im * p_im, c_re * p_im - c_im * p_re

    chips_here = 2 * tiles
    before = product(0)
    for c in range(chips_here):
        after = product(c + 1)
        both = jnp.concatenate([before[0] + after[0], before[1] + after[1]], axis=1)
        high, low = split(both)
        row, base = (c // 2) * FREQ, 2 * CHIP * (c % 2)
        zed[row:row + FREQ, base:base + 2 * CHIP] = high
        zed[row:row + FREQ, 4 * CHIP + base:4 * CHIP + base + 2 * CHIP] = low
        before = after
    both = zed[...]
    lags = dot(jnp.concatenate([both, both[:, :4 * CHIP]], axis=1), twice("back_columns"))
    pieces = [lags[t * FREQ:(t + 1) * FREQ] for t in range(tiles)]
    stacked = jnp.concatenate(
        [jnp.concatenate([piece[:, :LANES], piece[:, LANES:]], axis=0) for piece in pieces], axis=1)
    high, low = split(stacked)
    raw = dot(table("back_rows"), jnp.concatenate([high, low, high], axis=0))

    sums = jnp.concatenate([first, second], axis=0)
    sums = jnp.concatenate([sums[:, t * LANES:(t + 2) * LANES] for t in range(tiles)], axis=0)
    high, low = split(sums)
    boxes = dot(jnp.concatenate([high, low], axis=1), jnp.concatenate([table("slide")] * 2, axis=0))
    totals = jnp.concatenate(
        [jnp.sum(chips.reshape(CHIP // 8, 8, band), axis=0),
         jnp.sum((chips * chips).reshape(CHIP // 8, 8, band), axis=0)], axis=0)
    totals = jnp.concatenate([totals[:, t * LANES:(t + 2) * LANES] for t in range(tiles)], axis=0)
    high, low = split(totals)
    rest = (totals - high.astype(F32) - low.astype(F32)).astype(BF16)
    totals = dot(jnp.concatenate([high, low, rest], axis=1), jnp.concatenate([table("gather")] * 3, axis=0))

    scores = []
    for t in range(tiles):
        first_t = boxes[t * CHIP:t * CHIP + LAGS]
        second_t = boxes[t * CHIP + LAGS:(t + 1) * CHIP]
        total = jnp.sum(totals[16 * t:16 * t + 8], axis=0, keepdims=True)
        power = jnp.sum(totals[16 * t + 8:16 * t + 16], axis=0, keepdims=True)
        corr = raw[:, t * LANES:(t + 1) * LANES] - (total * (1.0 / AREA)) * first_t
        var_sum = second_t - first_t * first_t * (1.0 / AREA)
        energy = power - total * total * (1.0 / AREA)
        scores.append(CHIP * (corr * (1.0 / AREA)) * lax.rsqrt(
            (energy * (1.0 / AREA)) * (var_sum * (1.0 / AREA)) + EPSILON))
    high, low = split(jnp.concatenate(scores, axis=1))
    lifted = dot(table("cubic_rows"), jnp.concatenate([high, low], axis=0))
    lifted = jnp.concatenate([lifted[:, t * LANES:(t + 1) * LANES] for t in range(tiles)], axis=0)
    high, low = split(lifted)
    fine = dot(jnp.concatenate([high, low], axis=1), jnp.concatenate([table("cubic_cols")] * 2, axis=0))
    for c in range(chips_here):
        row, base = (c // 2) * CHIP, CHIP * (c % 2)
        out[0, c] = fine[row:row + CHIP, base:base + CHIP]


def neighbours(axis):
    size = lax.axis_size(axis)
    forth = [(i, i + 1) for i in range(size - 1)]
    return forth, [(j, i) for i, j in forth]


def body(ref_image, sec_image, off_az, off_rg):
    rows, cols = ref_image.shape
    side = CHIP // 4
    chip_rows, chip_cols = rows // SPACE, cols // SPACE
    all_rows = chip_rows * lax.axis_size("az")
    reach = min(SPACE - 1, (all_rows - 1) // 2)
    pad = -(-(SPACE + reach) // 8) * 8
    assert SPACE + reach + side <= LANES
    tiles = cols // LANES

    tall = rows + 2 * pad

    def full(*shape):
        return jax.ShapeDtypeStruct(shape, F32)

    away = pl.BlockSpec(memory_space=pltpu.MemorySpace.HBM)
    sec, ref, to_up, to_down, to_right, to_left = pl.pallas_call(
        functools.partial(pack_kernel, pad, side),
        in_specs=[away] * 2,
        out_shape=[full(rows, cols)] * 2 + [full(pad + side, cols)] * 2 + [full(rows, LANES)] * 2,
        scratch_shapes=[pltpu.SemaphoreType.DMA((6,))],
        compiler_params=pltpu.CompilerParams(vmem_limit_bytes=8 << 20),
    )(*(pltpu.with_memory_space_constraint(x, pltpu.MemorySpace.HBM) for x in (sec_image, ref_image)))
    forth, back = neighbours("az")
    east, west = neighbours("rg")
    up = lax.ppermute(to_up, "az", forth)
    down = lax.ppermute(to_down, "az", back)
    left = lax.ppermute(to_right, "rg", east)
    right = lax.ppermute(to_left, "rg", west)
    corners_up, corners_down = pl.pallas_call(
        functools.partial(corner_kernel, pad),
        out_shape=[full(pad, 2 * LANES)] * 2,
        compiler_params=pltpu.CompilerParams(vmem_limit_bytes=8 << 20),
    )(left, right)
    corner_up = lax.ppermute(corners_up, "az", forth)
    corner_down = lax.ppermute(corners_down, "az", back)

    slab = jnp.asarray(tables()[0])
    operands = [sec, ref, up, down, left, right, corner_up, corner_down]
    count = tiles + 1

    def whole(x):
        return pl.BlockSpec(x.shape, lambda i: (0, 0), pipeline_mode=pl.Buffered(1))

    return pl.pallas_call(
        functools.partial(main_kernel, pad, side),
        grid=(chip_rows,),
        in_specs=[away] * 3 + [whole(x) for x in operands],
        out_specs=pl.BlockSpec((1, chip_cols, 2 * LAGS, 2 * LAGS), lambda i: (i, 0, 0, 0)),
        scratch_shapes=[
            pltpu.VMEM(slab.shape, BF16),
            pltpu.SMEM((chip_rows,), jnp.int32),
            pltpu.SMEM((chip_rows,), jnp.int32),
            pltpu.VMEM((tall, cols + 2 * LANES), F32),
            pltpu.VMEM((rows + 2 * side, cols + LANES), F32),
            pltpu.VMEM((2 * count * FREQ, 4 * LANES), BF16),
            pltpu.VMEM((2 * count * FREQ, 4 * CHIP), F32),
            pltpu.VMEM((tiles * FREQ, 8 * CHIP), BF16),
            pltpu.SemaphoreType.DMA((3,)),
        ],
        out_shape=full(chip_rows, chip_cols, 2 * LAGS, 2 * LAGS),
        compiler_params=pltpu.CompilerParams(dimension_semantics=("arbitrary",), vmem_limit_bytes=40 << 20),
    )(*(pltpu.with_memory_space_constraint(x, pltpu.MemorySpace.HBM) for x in (off_az, off_rg, slab)), *operands)


def solution(mesh):
    return jax.shard_map(
        body,
        mesh=mesh,
        in_specs=(P("az", "rg"), P("az", "rg"), P("az"), P("az")),
        out_specs=P("az", "rg", None, None),
        check_vma=False,
    )
```

time: 53.7 us -> 39 us (0.73)
  local copies, waits for them, and re-layouts: 11.2 us -> 0 us
  waiting for transfers between devices: 16.1 us -> 8.01 us
  starting transfers between devices: 12 us -> 17.4 us
    unnamed x36 -> x0, local copies, waits for them, and re-layouts: 9.12 us -> none
    ppermute x4 -> x6, waiting for transfers between devices: 16.1 us -> 8.01 us  [the longest x1 4.06 us: body(): corner_down = lax.ppermute(corners_down, 'az', back)]
    ppermute x4 -> x6, starting transfers between devices: 12 us -> 17.4 us  [the longest x1 4.24 us: body(): left = lax.ppermute(to_right, 'rg', east)]
    slice x2 -> x0, local copies, waits for them, and re-layouts: 2.03 us -> none  [the longest x1 1.07 us: body(): sec_image[:pad]]
    pallas_call x2 -> x3, Pallas kernels: 13.4 us -> 13.2 us  [the longest x1 11.7 us: body(): pl.pallas_call(functools.partial(main_kernel, pad, side), grid=(chip_rows...]
  transfers between devices with their start and end apart: 4 -> 6, of which waited for: 3 -> 2; matrix products, arithmetic and copies ran while one was open for 0% -> 0% of each run, Pallas kernels for 0% -> 0%
where the time goes in v2:
time: 39 us; the launch traced here: 38.7 us
  starting transfers between devices  17.4 us (45%)
  Pallas kernels  13.2 us (34%)
  waiting for transfers between devices  8.01 us (21%)
    pallas_call x1, Pallas kernels, body(): pl.pallas_call(functools.partial(main_kernel, pad, side), grid=(chip_rows...  11.7 us
    ppermute x1, starting transfers between devices, body(): left = lax.ppermute(to_right, 'rg', east)  4.24 us
    ppermute x1, waiting for transfers between devices, body(): corner_down = lax.ppermute(corners_down, 'az', back)  4.06 us
    ppermute x1, starting transfers between devices, body(): corner_up = lax.ppermute(corners_up, 'az', forth)  4.05 us
    ppermute x1, waiting for transfers between devices, body(): right = lax.ppermute(to_left, 'rg', west)  3.94 us
    ppermute x1, starting transfers between devices, body(): up = lax.ppermute(to_up, 'az', forth)  3.15 us
    ppermute x1, starting transfers between devices, body(): down = lax.ppermute(to_down, 'az', back)  2.13 us
    ppermute x1, starting transfers between devices, body(): corner_down = lax.ppermute(corners_down, 'az', back)  1.92 us
  transfers between devices with their start and end apart: 6, of which 2 were waited for; matrix products, arithmetic and copies ran while one was open for 0% of the time, Pallas kernels for 0%

profile of v2, /device:TPU:21, one launch (start us, length us, event | category | flops | bytes accessed | tf_op | source)
XLA Modules:
  0.0 38.7 jit_solution(4514907108519567225)
XLA Ops:
  0.0 1.5 %shard_map.55 = (f32[128,768]{1,0:T(8,128)S(1)}, f32[128,768]{1,0:T(8,128)S(1)}, f32[104,768]{1,0:T(8,128)S(1)}, f32[104,768]{1,0:T(8,128)S(1)}, f32[128,128]{1,0:T(8,128)S(1)}, /*index=5*/f32[128,128]{1,0:T(8,128)S(1)}) custom-call(f32[128,768]{1,0:T(8,128)} %sec_hbm.1, f32[128,768]{1,0:T(8,128)} %ref_hbm.1), custom_call_target="tpu_custom_call" | custom-call | tf_op jit(solution)/shard_map/pallas_call | solution.py:312
  1.5 3.1 %collective-permute-start = (f32[104,768]{1,0:T(8,128)S(1)}, f32[104,768]{1,0:T(8,128)S(1)}, u32[]{:S(2)}, u32[]{:S(2)}) collective-permute-start(f32[104,768]{1,0:T(8,128)S(1)} %get-tuple-element.15), channel_id=1, source_target_pairs={{0,4},{4,8},{8,12},{12,16},{16,20},{20,24},{24,28},{1,5},{5,9},{9,... | collective-permute-start | bytes 958472 | tf_op jit(solution)/shard_map/ppermute | solution.py:321
  4.6 2.1 %collective-permute-start.1 = (f32[104,768]{1,0:T(8,128)S(1)}, f32[104,768]{1,0:T(8,128)S(1)}, u32[]{:S(2)}, u32[]{:S(2)}) collective-permute-start(f32[104,768]{1,0:T(8,128)S(1)} %get-tuple-element.16), channel_id=1, source_target_pairs={{4,0},{8,4},{12,8},{16,12},{20,16},{24,20},{28,24},{5,1},{9,5},{13... | collective-permute-start | bytes 958472 | tf_op jit(solution)/shard_map/ppermute | solution.py:322
  6.8 4.2 %collective-permute-start.2 = (f32[128,128]{1,0:T(8,128)S(1)}, f32[128,128]{1,0:T(8,128)S(1)}, u32[]{:S(2)}, u32[]{:S(2)}) collective-permute-start(f32[128,128]{1,0:T(8,128)S(1)} %get-tuple-element.17), channel_id=1, source_target_pairs={{0,1},{1,2},{2,3},{4,5},{5,6},{6,7},{8,9},{9,10},{10,11},{12,13},{... | collective-permute-start | bytes 196616 | tf_op jit(solution)/shard_map/ppermute | solution.py:323
  11.0 1.9 %collective-permute-start.3 = (f32[128,128]{1,0:T(8,128)S(1)}, f32[128,128]{1,0:T(8,128)S(1)}, u32[]{:S(2)}, u32[]{:S(2)}) collective-permute-start(f32[128,128]{1,0:T(8,128)S(1)} %get-tuple-element.18), channel_id=1, source_target_pairs={{1,0},{2,1},{3,2},{5,4},{6,5},{7,6},{9,8},{10,9},{11,10},{13,12},{... | collective-permute-start | bytes 196616 | tf_op jit(solution)/shard_map/ppermute | solution.py:324
  12.9 0.0 collective-permute-done.2.left
  12.9 3.9 %collective-permute-done.3.right = f32[128,128]{1,0:T(8,128)S(1)} collective-permute-done((f32[128,128]{1,0:T(8,128)S(1)}, f32[128,128]{1,0:T(8,128)S(1)}, u32[]{:S(2)}, u32[]{:S(2)}) %collective-permute-start.3) | collective-permute-done | bytes 65568 | tf_op jit(solution)/shard_map/ppermute | solution.py:324
  16.9 4.0 %collective-permute-start.4 = (f32[72,256]{1,0:T(8,128)S(1)}, f32[72,256]{1,0:T(8,128)S(1)}, u32[]{:S(2)}, u32[]{:S(2)}) collective-permute-start(f32[72,256]{1,0:T(8,128)S(1)} %get-tuple-element.19), channel_id=1, source_target_pairs={{0,4},{4,8},{8,12},{12,16},{16,20},{20,24},{24,28},{1,5},{5,9},{9,... | collective-permute-start | bytes 221192 | tf_op jit(solution)/shard_map/ppermute | solution.py:330
  21.0 1.9 %collective-permute-start.5 = (f32[72,256]{1,0:T(8,128)S(1)}, f32[72,256]{1,0:T(8,128)S(1)}, u32[]{:S(2)}, u32[]{:S(2)}) collective-permute-start(f32[72,256]{1,0:T(8,128)S(1)} %get-tuple-element.20), channel_id=1, source_target_pairs={{4,0},{8,4},{12,8},{16,12},{20,16},{24,20},{28,24},{5,1},{9,5},{13... | collective-permute-start | bytes 221192 | tf_op jit(solution)/shard_map/ppermute | solution.py:331
  22.9 0.0 collective-permute-done.4.corner_up
  22.9 4.1 %collective-permute-done.5.corner_down = f32[72,256]{1,0:T(8,128)S(1)} collective-permute-done((f32[72,256]{1,0:T(8,128)S(1)}, f32[72,256]{1,0:T(8,128)S(1)}, u32[]{:S(2)}, u32[]{:S(2)}) %collective-permute-start.5) | collective-permute-done | bytes 73760 | tf_op jit(solution)/shard_map/ppermute | solution.py:331
  27.0 0.0 collective-permute-done.up
  27.0 0.0 collective-permute-done.1.down
  27.0 11.7 %shard_map.57 = f32[2,12,128,128]{3,2,1,0:T(8,128)} custom-call(s32[2]{0:T(128)} %off_az_hbm.1, s32[2]{0:T(128)} %off_rg_hbm.1, bf16[7360,128]{1,0:T(8,128)(2,1)} %constant.2.clone.slab_hbm, f32[128,768]{1,0:T(8,128)S(1)} %get-tuple-element.13.sec, f32[128,768]{1,0:T(8,128)S(1)} %get-tuple-element.14.ref, f32[104,768]{1,0:T(8,128)S(1)} %collective-permute-done.up, ...), custom_call_target="tpu_custom_call" | custom-call | tf_op jit(solution)/shard_map/pallas_call | solution.py:340
  (1 shorter events, 0.0 us)
Async XLA Ops:
  1.5 25.5 %collective-permute-start = (f32[104,768]{1,0:T(8,128)S(1)}, f32[104,768]{1,0:T(8,128)S(1)}, u32[]{:S(2)}, u32[]{:S(2)}) collective-permute-start(f32[104,768]{1,0:T(8,128)S(1)} %get-tuple-element.15), channel_id=1, source_target_pairs={{0,4},{4,8},{8,12},{12,16},{16,20},{20,24},{24,28},{1,5},{5,9},{9,... | collective-permute-start | bytes 958472 | tf_op jit(solution)/shard_map/ppermute | solution.py:321
  4.6 22.3 %collective-permute-start.1 = (f32[104,768]{1,0:T(8,128)S(1)}, f32[104,768]{1,0:T(8,128)S(1)}, u32[]{:S(2)}, u32[]{:S(2)}) collective-permute-start(f32[104,768]{1,0:T(8,128)S(1)} %get-tuple-element.16), channel_id=1, source_target_pairs={{4,0},{8,4},{12,8},{16,12},{20,16},{24,20},{28,24},{5,1},{9,5},{13... | collective-permute-start | bytes 958472 | tf_op jit(solution)/shard_map/ppermute | solution.py:322
  6.8 6.2 %collective-permute-start.2 = (f32[128,128]{1,0:T(8,128)S(1)}, f32[128,128]{1,0:T(8,128)S(1)}, u32[]{:S(2)}, u32[]{:S(2)}) collective-permute-start(f32[128,128]{1,0:T(8,128)S(1)} %get-tuple-element.17), channel_id=1, source_target_pairs={{0,1},{1,2},{2,3},{4,5},{5,6},{6,7},{8,9},{9,10},{10,11},{12,13},{... | collective-permute-start | bytes 196616 | tf_op jit(solution)/shard_map/ppermute | solution.py:323
  11.0 5.9 %collective-permute-start.3 = (f32[128,128]{1,0:T(8,128)S(1)}, f32[128,128]{1,0:T(8,128)S(1)}, u32[]{:S(2)}, u32[]{:S(2)}) collective-permute-start(f32[128,128]{1,0:T(8,128)S(1)} %get-tuple-element.18), channel_id=1, source_target_pairs={{1,0},{2,1},{3,2},{5,4},{6,5},{7,6},{9,8},{10,9},{11,10},{13,12},{... | collective-permute-start | bytes 196616 | tf_op jit(solution)/shard_map/ppermute | solution.py:324
  16.9 6.0 %collective-permute-start.4 = (f32[72,256]{1,0:T(8,128)S(1)}, f32[72,256]{1,0:T(8,128)S(1)}, u32[]{:S(2)}, u32[]{:S(2)}) collective-permute-start(f32[72,256]{1,0:T(8,128)S(1)} %get-tuple-element.19), channel_id=1, source_target_pairs={{0,4},{4,8},{8,12},{12,16},{16,20},{20,24},{24,28},{1,5},{5,9},{9,... | collective-permute-start | bytes 221192 | tf_op jit(solution)/shard_map/ppermute | solution.py:330
  21.0 6.0 %collective-permute-start.5 = (f32[72,256]{1,0:T(8,128)S(1)}, f32[72,256]{1,0:T(8,128)S(1)}, u32[]{:S(2)}, u32[]{:S(2)}) collective-permute-start(f32[72,256]{1,0:T(8,128)S(1)} %get-tuple-element.20), channel_id=1, source_target_pairs={{4,0},{8,4},{12,8},{16,12},{20,16},{24,20},{28,24},{5,1},{9,5},{13... | collective-permute-start | bytes 221192 | tf_op jit(solution)/shard_map/ppermute | solution.py:331

commit v3 on v2

--- a/solution.py
+++ b/solution.py
@@ -8,6 +8,7 @@
 from jax.experimental import pallas as pl
 from jax.experimental.pallas import tpu as pltpu
 from jax.sharding import PartitionSpec as P
+
 
 CHIP = 128
 SPACE = 64
@@ -45,22 +46,12 @@
     spot = np.arange(SPACE)[:, None]
     cosine, sine = np.cos(phi * spot), np.sin(phi * spot)
     parts = (np.concatenate([cosine, -sine], axis=1), np.concatenate([sine, cosine], axis=1))
-    spread = np.zeros((4 * SPACE, 4 * CHIP))
-    for half in range(2):
-        for part in range(2):
-            row = 2 * SPACE * part + SPACE * half
-            spread[row:row + SPACE, 2 * CHIP * half:2 * CHIP * (half + 1)] = parts[part]
-    made["columns"] = np.concatenate(halves(spread), axis=0)
-
-    back = np.zeros((4 * CHIP, 4 * LAGS))
+    made["columns"] = np.concatenate(halves(np.concatenate(parts, axis=0)), axis=0)
+
     cosine, sine = np.cos(phi.T * lag.T), np.sin(phi.T * lag.T)
-    for half in range(2):
-        base = 2 * CHIP * half
-        back[base:base + CHIP, LAGS * half:LAGS * (half + 1)] = cosine
-        back[base:base + CHIP, LAGS * (2 + half):LAGS * (3 + half)] = sine
-        back[base + CHIP:base + 2 * CHIP, LAGS * half:LAGS * (half + 1)] = -sine
-        back[base + CHIP:base + 2 * CHIP, LAGS * (2 + half):LAGS * (3 + half)] = cosine
-    made["back_columns"] = np.concatenate(halves(back), axis=0)
+    back = np.concatenate(
+        [np.concatenate([cosine, sine], axis=1), np.concatenate([-sine, cosine], axis=1)], axis=0)
+    made["back_columns"] = np.concatenate(halves(back), axis=1)
 
     final = np.concatenate([np.cos(theta.T * lag), -np.sin(theta.T * lag)], axis=1)
     high, low = halves(final * (2.0 / (SEARCH * CHIP)))
@@ -144,7 +135,6 @@
     rows, cols = sec.shape
     tiles = cols // LANES
     step = pl.program_id(0)
-    width = cols + 2 * LANES
     band = cols + LANES
 
     def table(name):
@@ -152,11 +142,6 @@
         pieces = [slab[top + i * height:top + (i + 1) * height, :] for i in range(count)]
         value = jnp.concatenate(pieces, axis=1) if count > 1 else pieces[0]
         return value[:, :last]
-
-    def twice(name):
-        value = table(name)
-        half = value.shape[0] // 2
-        return jnp.concatenate([value[:half], value], axis=0)
 
     @pl.when(step == 0)
     def _():
@@ -196,6 +181,30 @@
         for copy in copies:
             copy.wait()
 
+    count = tiles + 1
+
+    lane = lax.broadcasted_iota(jnp.int32, (1, LANES), 1)
+    both = table("columns")
+    major, minor = jnp.concatenate([both[:LANES]] * 2, axis=0), both[LANES:]
+
+    def spread(which, source):
+        for t in range(count):
+            here = slice(t * LANES, (t + 1) * LANES)
+            real, imag = source[:FREQ, here], source[FREQ:2 * FREQ, here]
+            even = jnp.where(lane < SPACE, real, pltpu.roll(imag, SPACE, 1))
+            odd = jnp.where(lane < SPACE, pltpu.roll(real, SPACE, 1), imag)
+            for i, value in enumerate((even, odd)):
+                row = ((which * count + t) * 2 + i) * FREQ
+                lhs[row:row + FREQ, :] = jnp.concatenate(split(value), axis=1)
+        for i in range(2):
+            low = (which * 2 + i) * count * FREQ
+            here = slice(low, low + count * FREQ)
+            spec[here, :] = dot(lhs[here, :], major) + dot(lhs[here, :LANES], minor)
+
+    chips = ref_ext[pl.ds(pl.multiple_of(step * SPACE, SPACE), CHIP), :]
+    high, low = split(chips)
+    spread(1, dot(table("rows_ref"), jnp.concatenate([high, low, high], axis=0)))
+
     start = step * SPACE + (pad - SPACE) + off_az[step]
     aligned = pl.multiple_of(start // 8 * 8, 8)
     field = sec_ext[pl.ds(aligned, SEARCH + 8), :]
@@ -204,32 +213,22 @@
     lane = lax.broadcasted_iota(jnp.int32, (1, LANES), 1)
     field = jnp.concatenate(
         [jnp.where(lane < shift, turned[t], turned[t + 1]) for t in range(tiles + 1)], axis=1)
-    field = pltpu.roll(field, SEARCH + 8 - (start - aligned), 0)[:SEARCH]
+    part = start - aligned
+    field = pltpu.roll(field.reshape(SEARCH // 8 + 1, 8, band), 8 - part, 1)
+    line = lax.broadcasted_iota(jnp.int32, (1, 8, 1), 1)
+    field = jnp.where(line < 8 - part, field[:-1], field[1:]).reshape(SEARCH, band)
     high, low = split(field)
     spectrum = dot(table("rows_sec"), jnp.concatenate([high, low, high], axis=0))
     square_high, square_low = split(field * field)
     second = dot(table("rows_box"), jnp.concatenate([square_high, square_low], axis=0))
     first = spectrum[2 * FREQ:]
-    chips = ref_ext[pl.ds(pl.multiple_of(step * SPACE, SPACE), CHIP), :]
-    high, low = split(chips)
-    chip_spectrum = dot(table("rows_ref"), jnp.concatenate([high, low, high], axis=0))
-    count = tiles + 1
-    for which, source in enumerate((spectrum, chip_spectrum)):
-        for t in range(count):
-            here = slice(t * LANES, (t + 1) * LANES)
-            both = jnp.concatenate([source[:FREQ, here], source[FREQ:2 * FREQ, here]], axis=1)
-            high, low = split(both)
-            row = (which * count + t) * FREQ
-            lhs[row:row + FREQ, :] = jnp.concatenate([high, low], axis=1)
-    both = lhs[...]
-    spec[...] = dot(jnp.concatenate([both, both[:, :2 * LANES]], axis=1), twice("columns"))
+    spread(0, spectrum)
 
     sign = (1 - 2 * (lax.broadcasted_iota(jnp.int32, (1, LANES), 1) % 2)).astype(F32)
 
     def block(which, b):
-        row = (which * count + b // 2) * FREQ
-        base = 2 * CHIP * (b % 2)
-        return spec[row:row + FREQ, base:base + CHIP], spec[row:row + FREQ, base + CHIP:base + 2 * CHIP]
+        row = (which * count * 2 + b) * FREQ
+        return spec[row:row + FREQ, :CHIP], spec[row:row + FREQ, CHIP:]
 
     def product(b):
         (w_re, w_im), (n_re, n_im), (c_re, c_im) = block(0, b), block(0, b + 1), block(1, b)
@@ -242,22 +241,34 @@
         after = product(c + 1)
         both = jnp.concatenate([before[0] + after[0], before[1] + after[1]], axis=1)
         high, low = split(both)
-        row, base = (c // 2) * FREQ, 2 * CHIP * (c % 2)
-        zed[row:row + FREQ, base:base + 2 * CHIP] = high
-        zed[row:row + FREQ, 4 * CHIP + base:4 * CHIP + base + 2 * CHIP] = low
+        row = c * FREQ
+        zed[row:row + FREQ, :2 * CHIP] = high
+        zed[row:row + FREQ, 2 * CHIP:] = low
         before = after
-    both = zed[...]
-    lags = dot(jnp.concatenate([both, both[:, :4 * CHIP]], axis=1), twice("back_columns"))
-    pieces = [lags[t * FREQ:(t + 1) * FREQ] for t in range(tiles)]
-    stacked = jnp.concatenate(
-        [jnp.concatenate([piece[:, :LANES], piece[:, LANES:]], axis=0) for piece in pieces], axis=1)
+    back = table("back_columns")
+    main = dot(zed[:, :2 * CHIP], back)
+    rest = dot(zed[:, 2 * CHIP:], back[:, :2 * LAGS])
+    pieces = []
+    for t in range(tiles):
+        pair = []
+        for row in (2 * t * FREQ, (2 * t + 1) * FREQ):
+            here = main[row:row + FREQ]
+            pair.append(here[:, :LANES] + here[:, LANES:] + rest[row:row + FREQ])
+        even, odd = pair[0], pair[1]
+        odd_turned, even_turned = pltpu.roll(odd, LAGS, 1), pltpu.roll(even, LAGS, 1)
+        pieces.append(jnp.concatenate(
+            [jnp.where(lane < LAGS, even, odd_turned), jnp.where(lane < LAGS, even_turned, odd)], axis=0))
+    stacked = jnp.concatenate(pieces, axis=1)
     high, low = split(stacked)
     raw = dot(table("back_rows"), jnp.concatenate([high, low, high], axis=0))
 
-    sums = jnp.concatenate([first, second], axis=0)
-    sums = jnp.concatenate([sums[:, t * LANES:(t + 2) * LANES] for t in range(tiles)], axis=0)
-    high, low = split(sums)
-    boxes = dot(jnp.concatenate([high, low], axis=1), jnp.concatenate([table("slide")] * 2, axis=0))
+    slide = jnp.concatenate([table("slide")] * 2, axis=0)
+
+    def boxes(sums):
+        sums = jnp.concatenate([sums[:, t * LANES:(t + 2) * LANES] for t in range(tiles)], axis=0)
+        return dot(jnp.concatenate(split(sums), axis=1), slide)
+
+    firsts, seconds = boxes(first), boxes(second)
     totals = jnp.concatenate(
         [jnp.sum(chips.reshape(CHIP // 8, 8, band), axis=0),
          jnp.sum((chips * chips).reshape(CHIP // 8, 8, band), axis=0)], axis=0)
@@ -268,8 +279,8 @@
 
     scores = []
     for t in range(tiles):
-        first_t = boxes[t * CHIP:t * CHIP + LAGS]
-        second_t = boxes[t * CHIP + LAGS:(t + 1) * CHIP]
+        first_t = firsts[t * LAGS:(t + 1) * LAGS]
+        second_t = seconds[t * LAGS:(t + 1) * LAGS]
         total = jnp.sum(totals[16 * t:16 * t + 8], axis=0, keepdims=True)
         power = jnp.sum(totals[16 * t + 8:16 * t + 16], axis=0, keepdims=True)
         corr = raw[:, t * LANES:(t + 1) * LANES] - (total * (1.0 / AREA)) * first_t
@@ -279,12 +290,15 @@
             (energy * (1.0 / AREA)) * (var_sum * (1.0 / AREA)) + EPSILON))
     high, low = split(jnp.concatenate(scores, axis=1))
     lifted = dot(table("cubic_rows"), jnp.concatenate([high, low], axis=0))
-    lifted = jnp.concatenate([lifted[:, t * LANES:(t + 1) * LANES] for t in range(tiles)], axis=0)
-    high, low = split(lifted)
-    fine = dot(jnp.concatenate([high, low], axis=1), jnp.concatenate([table("cubic_cols")] * 2, axis=0))
-    for c in range(chips_here):
-        row, base = (c // 2) * CHIP, CHIP * (c % 2)
-        out[0, c] = fine[row:row + CHIP, base:base + CHIP]
+    cubic = jnp.concatenate([table("cubic_cols")] * 2, axis=0)
+    half = (tiles + 1) // 2
+    for begin, end in ((0, half), (half, tiles)):
+        part = jnp.concatenate([lifted[:, t * LANES:(t + 1) * LANES] for t in range(begin, end)], axis=0)
+        fine = dot(jnp.concatenate(split(part), axis=1), cubic)
+        for t in range(begin, end):
+            row = (t - begin) * CHIP
+            out[0, 2 * t] = fine[row:row + CHIP, :CHIP]
+            out[0, 2 * t + 1] = fine[row:row + CHIP, CHIP:]
 
 
 def neighbours(axis):
@@ -348,9 +362,9 @@
             pltpu.SMEM((chip_rows,), jnp.int32),
             pltpu.VMEM((tall, cols + 2 * LANES), F32),
             pltpu.VMEM((rows + 2 * side, cols + LANES), F32),
-            pltpu.VMEM((2 * count * FREQ, 4 * LANES), BF16),
-            pltpu.VMEM((2 * count * FREQ, 4 * CHIP), F32),
-            pltpu.VMEM((tiles * FREQ, 8 * CHIP), BF16),
+            pltpu.VMEM((4 * count * FREQ, 2 * LANES), BF16),
+            pltpu.VMEM((4 * count * FREQ, 2 * CHIP), F32),
+            pltpu.VMEM((chip_cols * FREQ, 4 * CHIP), BF16),
             pltpu.SemaphoreType.DMA((3,)),
         ],
         out_shape=full(chip_rows, chip_cols, 2 * LAGS, 2 * LAGS),

time: 39 us -> 36.1 us (0.926)
  Pallas kernels: 13.2 us -> 10.3 us
    pallas_call x1, Pallas kernels: 11.7 us -> 8.97 us  [body(): pl.pallas_call(functools.partial(main_kernel, pad, side), grid=(chip_rows...]
where the time goes in v3:
time: 36.1 us; the launch traced here: 35.8 us
  starting transfers between devices  17.4 us (48%)
  Pallas kernels  10.3 us (29%)
  waiting for transfers between devices  8.01 us (22%)
    pallas_call x1, Pallas kernels, body(): pl.pallas_call(functools.partial(main_kernel, pad, side), grid=(chip_rows...  8.97 us
    ppermute x1, starting transfers between devices, body(): left = lax.ppermute(to_right, 'rg', east)  4.24 us
    ppermute x1, waiting for transfers between devices, body(): corner_down = lax.ppermute(corners_down, 'az', back)  4.06 us
    ppermute x1, starting transfers between devices, body(): corner_up = lax.ppermute(corners_up, 'az', forth)  4.05 us
    ppermute x1, waiting for transfers between devices, body(): right = lax.ppermute(to_left, 'rg', west)  3.94 us
    ppermute x1, starting transfers between devices, body(): up = lax.ppermute(to_up, 'az', forth)  3.15 us
    ppermute x1, starting transfers between devices, body(): down = lax.ppermute(to_down, 'az', back)  2.13 us
    ppermute x1, starting transfers between devices, body(): right = lax.ppermute(to_left, 'rg', west)  1.92 us
  transfers between devices with their start and end apart: 6, of which 2 were waited for; matrix products, arithmetic and copies ran while one was open for 0% of the time, Pallas kernels for 0%

profile of v3, /device:TPU:21, one launch (start us, length us, event | category | flops | bytes accessed | tf_op | source)
XLA Modules:
  0.0 35.8 jit_solution(13348024637122533552)
XLA Ops:
  0.0 1.3 %shard_map.55 = (f32[128,768]{1,0:T(8,128)S(1)}, f32[128,768]{1,0:T(8,128)S(1)}, f32[104,768]{1,0:T(8,128)S(1)}, f32[104,768]{1,0:T(8,128)S(1)}, f32[128,128]{1,0:T(8,128)S(1)}, /*index=5*/f32[128,128]{1,0:T(8,128)S(1)}) custom-call(f32[128,768]{1,0:T(8,128)} %sec_hbm.1, f32[128,768]{1,0:T(8,128)} %ref_hbm.1), custom_call_target="tpu_custom_call" | custom-call | tf_op jit(solution)/shard_map/pallas_call | solution.py:326
  1.4 3.1 %collective-permute-start = (f32[104,768]{1,0:T(8,128)S(1)}, f32[104,768]{1,0:T(8,128)S(1)}, u32[]{:S(2)}, u32[]{:S(2)}) collective-permute-start(f32[104,768]{1,0:T(8,128)S(1)} %get-tuple-element.15), channel_id=1, source_target_pairs={{0,4},{4,8},{8,12},{12,16},{16,20},{20,24},{24,28},{1,5},{5,9},{9,... | collective-permute-start | bytes 958472 | tf_op jit(solution)/shard_map/ppermute | solution.py:335
  4.5 2.1 %collective-permute-start.1 = (f32[104,768]{1,0:T(8,128)S(1)}, f32[104,768]{1,0:T(8,128)S(1)}, u32[]{:S(2)}, u32[]{:S(2)}) collective-permute-start(f32[104,768]{1,0:T(8,128)S(1)} %get-tuple-element.16), channel_id=1, source_target_pairs={{4,0},{8,4},{12,8},{16,12},{20,16},{24,20},{28,24},{5,1},{9,5},{13... | collective-permute-start | bytes 958472 | tf_op jit(solution)/shard_map/ppermute | solution.py:336
  6.6 4.2 %collective-permute-start.2 = (f32[128,128]{1,0:T(8,128)S(1)}, f32[128,128]{1,0:T(8,128)S(1)}, u32[]{:S(2)}, u32[]{:S(2)}) collective-permute-start(f32[128,128]{1,0:T(8,128)S(1)} %get-tuple-element.17), channel_id=1, source_target_pairs={{0,1},{1,2},{2,3},{4,5},{5,6},{6,7},{8,9},{9,10},{10,11},{12,13},{... | collective-permute-start | bytes 196616 | tf_op jit(solution)/shard_map/ppermute | solution.py:337
  10.9 1.9 %collective-permute-start.3 = (f32[128,128]{1,0:T(8,128)S(1)}, f32[128,128]{1,0:T(8,128)S(1)}, u32[]{:S(2)}, u32[]{:S(2)}) collective-permute-start(f32[128,128]{1,0:T(8,128)S(1)} %get-tuple-element.18), channel_id=1, source_target_pairs={{1,0},{2,1},{3,2},{5,4},{6,5},{7,6},{9,8},{10,9},{11,10},{13,12},{... | collective-permute-start | bytes 196616 | tf_op jit(solution)/shard_map/ppermute | solution.py:338
  12.8 0.0 collective-permute-done.2.left
  12.8 3.9 %collective-permute-done.3.right = f32[128,128]{1,0:T(8,128)S(1)} collective-permute-done((f32[128,128]{1,0:T(8,128)S(1)}, f32[128,128]{1,0:T(8,128)S(1)}, u32[]{:S(2)}, u32[]{:S(2)}) %collective-permute-start.3) | collective-permute-done | bytes 65568 | tf_op jit(solution)/shard_map/ppermute | solution.py:338
  16.8 4.0 %collective-permute-start.4 = (f32[72,256]{1,0:T(8,128)S(1)}, f32[72,256]{1,0:T(8,128)S(1)}, u32[]{:S(2)}, u32[]{:S(2)}) collective-permute-start(f32[72,256]{1,0:T(8,128)S(1)} %get-tuple-element.19), channel_id=1, source_target_pairs={{0,4},{4,8},{8,12},{12,16},{16,20},{20,24},{24,28},{1,5},{5,9},{9,... | collective-permute-start | bytes 221192 | tf_op jit(solution)/shard_map/ppermute | solution.py:344
  20.8 1.9 %collective-permute-start.5 = (f32[72,256]{1,0:T(8,128)S(1)}, f32[72,256]{1,0:T(8,128)S(1)}, u32[]{:S(2)}, u32[]{:S(2)}) collective-permute-start(f32[72,256]{1,0:T(8,128)S(1)} %get-tuple-element.20), channel_id=1, source_target_pairs={{4,0},{8,4},{12,8},{16,12},{20,16},{24,20},{28,24},{5,1},{9,5},{13... | collective-permute-start | bytes 221192 | tf_op jit(solution)/shard_map/ppermute | solution.py:345
  22.8 0.0 collective-permute-done.4.corner_up
  22.8 4.1 %collective-permute-done.5.corner_down = f32[72,256]{1,0:T(8,128)S(1)} collective-permute-done((f32[72,256]{1,0:T(8,128)S(1)}, f32[72,256]{1,0:T(8,128)S(1)}, u32[]{:S(2)}, u32[]{:S(2)}) %collective-permute-start.5) | collective-permute-done | bytes 73760 | tf_op jit(solution)/shard_map/ppermute | solution.py:345
  26.8 0.0 collective-permute-done.up
  26.8 0.0 collective-permute-done.1.down
  26.8 9.0 %shard_map.57 = f32[2,12,128,128]{3,2,1,0:T(8,128)} custom-call(s32[2]{0:T(128)} %off_az_hbm.1, s32[2]{0:T(128)} %off_rg_hbm.1, bf16[4288,128]{1,0:T(8,128)(2,1)} %constant.2.clone.slab_hbm, f32[128,768]{1,0:T(8,128)S(1)} %get-tuple-element.13.sec, f32[128,768]{1,0:T(8,128)S(1)} %get-tuple-element.14.ref, f32[104,768]{1,0:T(8,128)S(1)} %collective-permute-done.up, ...), custom_call_target="tpu_custom_call" | custom-call | tf_op jit(solution)/shard_map/pallas_call | solution.py:354
  (1 shorter events, 0.0 us)
Async XLA Ops:
  1.4 25.5 %collective-permute-start = (f32[104,768]{1,0:T(8,128)S(1)}, f32[104,768]{1,0:T(8,128)S(1)}, u32[]{:S(2)}, u32[]{:S(2)}) collective-permute-start(f32[104,768]{1,0:T(8,128)S(1)} %get-tuple-element.15), channel_id=1, source_target_pairs={{0,4},{4,8},{8,12},{12,16},{16,20},{20,24},{24,28},{1,5},{5,9},{9,... | collective-permute-start | bytes 958472 | tf_op jit(solution)/shard_map/ppermute | solution.py:335
  4.5 22.3 %collective-permute-start.1 = (f32[104,768]{1,0:T(8,128)S(1)}, f32[104,768]{1,0:T(8,128)S(1)}, u32[]{:S(2)}, u32[]{:S(2)}) collective-permute-start(f32[104,768]{1,0:T(8,128)S(1)} %get-tuple-element.16), channel_id=1, source_target_pairs={{4,0},{8,4},{12,8},{16,12},{20,16},{24,20},{28,24},{5,1},{9,5},{13... | collective-permute-start | bytes 958472 | tf_op jit(solution)/shard_map/ppermute | solution.py:336
  6.6 6.2 %collective-permute-start.2 = (f32[128,128]{1,0:T(8,128)S(1)}, f32[128,128]{1,0:T(8,128)S(1)}, u32[]{:S(2)}, u32[]{:S(2)}) collective-permute-start(f32[128,128]{1,0:T(8,128)S(1)} %get-tuple-element.17), channel_id=1, source_target_pairs={{0,1},{1,2},{2,3},{4,5},{5,6},{6,7},{8,9},{9,10},{10,11},{12,13},{... | collective-permute-start | bytes 196616 | tf_op jit(solution)/shard_map/ppermute | solution.py:337
  10.9 5.9 %collective-permute-start.3 = (f32[128,128]{1,0:T(8,128)S(1)}, f32[128,128]{1,0:T(8,128)S(1)}, u32[]{:S(2)}, u32[]{:S(2)}) collective-permute-start(f32[128,128]{1,0:T(8,128)S(1)} %get-tuple-element.18), channel_id=1, source_target_pairs={{1,0},{2,1},{3,2},{5,4},{6,5},{7,6},{9,8},{10,9},{11,10},{13,12},{... | collective-permute-start | bytes 196616 | tf_op jit(solution)/shard_map/ppermute | solution.py:338
  16.8 6.0 %collective-permute-start.4 = (f32[72,256]{1,0:T(8,128)S(1)}, f32[72,256]{1,0:T(8,128)S(1)}, u32[]{:S(2)}, u32[]{:S(2)}) collective-permute-start(f32[72,256]{1,0:T(8,128)S(1)} %get-tuple-element.19), channel_id=1, source_target_pairs={{0,4},{4,8},{8,12},{12,16},{16,20},{20,24},{24,28},{1,5},{5,9},{9,... | collective-permute-start | bytes 221192 | tf_op jit(solution)/shard_map/ppermute | solution.py:344
  20.8 6.0 %collective-permute-start.5 = (f32[72,256]{1,0:T(8,128)S(1)}, f32[72,256]{1,0:T(8,128)S(1)}, u32[]{:S(2)}, u32[]{:S(2)}) collective-permute-start(f32[72,256]{1,0:T(8,128)S(1)} %get-tuple-element.20), channel_id=1, source_target_pairs={{4,0},{8,4},{12,8},{16,12},{20,16},{24,20},{28,24},{5,1},{9,5},{13... | collective-permute-start | bytes 221192 | tf_op jit(solution)/shard_map/ppermute | solution.py:345

commit v4 on v3

--- a/solution.py
+++ b/solution.py
@@ -130,8 +130,14 @@
     down[:, LANES:] = right[:pad]
 
 
-def main_kernel(pad, side, off_az_hbm, off_rg_hbm, slab_hbm, sec, ref, up, down, left, right, corner_up,
-                corner_down, out, slab, off_az, off_rg, sec_ext, ref_ext, lhs, spec, zed, sems):
+def fetch_kernel(source, target, sem):
+    copy = pltpu.make_async_copy(source, target, sem)
+    copy.start()
+    copy.wait()
+
+
+def main_kernel(pad, side, off_az_hbm, off_rg_hbm, slab, sec, ref, up, down, left, right, corner_up,
+                corner_down, out, off_az, off_rg, sec_ext, ref_ext, lhs, spec, zed, sems):
     rows, cols = sec.shape
     tiles = cols // LANES
     step = pl.program_id(0)
@@ -148,7 +154,7 @@
         copies = [
             pltpu.make_async_copy(source, target, sems.at[i])
             for i, (source, target) in enumerate(
-                [(slab_hbm, slab), (off_az_hbm, off_az), (off_rg_hbm, off_rg)])
+                [(off_az_hbm, off_az), (off_rg_hbm, off_rg)])
         ]
         for copy in copies:
             copy.start()
@@ -345,7 +351,14 @@
     corner_down = lax.ppermute(corners_down, "az", back)
 
     slab = jnp.asarray(tables()[0])
-    operands = [sec, ref, up, down, left, right, corner_up, corner_down]
+    held = pl.pallas_call(
+        fetch_kernel,
+        in_specs=[away],
+        out_shape=jax.ShapeDtypeStruct(slab.shape, BF16),
+        scratch_shapes=[pltpu.SemaphoreType.DMA],
+        compiler_params=pltpu.CompilerParams(vmem_limit_bytes=8 << 20),
+    )(pltpu.with_memory_space_constraint(slab, pltpu.MemorySpace.HBM))
+    operands = [held, sec, ref, up, down, left, right, corner_up, corner_down]
     count = tiles + 1
 
     def whole(x):
@@ -354,10 +367,9 @@
     return pl.pallas_call(
         functools.partial(main_kernel, pad, side),
         grid=(chip_rows,),
-        in_specs=[away] * 3 + [whole(x) for x in operands],
+        in_specs=[away] * 2 + [whole(x) for x in operands],
         out_specs=pl.BlockSpec((1, chip_cols, 2 * LAGS, 2 * LAGS), lambda i: (i, 0, 0, 0)),
         scratch_shapes=[
-            pltpu.VMEM(slab.shape, BF16),
             pltpu.SMEM((chip_rows,), jnp.int32),
             pltpu.SMEM((chip_rows,), jnp.int32),
             pltpu.VMEM((tall, cols + 2 * LANES), F32),
@@ -369,7 +381,7 @@
         ],
         out_shape=full(chip_rows, chip_cols, 2 * LAGS, 2 * LAGS),
         compiler_params=pltpu.CompilerParams(dimension_semantics=("arbitrary",), vmem_limit_bytes=40 << 20),
-    )(*(pltpu.with_memory_space_constraint(x, pltpu.MemorySpace.HBM) for x in (off_az, off_rg, slab)), *operands)
+    )(*(pltpu.with_memory_space_constraint(x, pltpu.MemorySpace.HBM) for x in (off_az, off_rg)), *operands)
 
 
 def solution(mesh):

time: 36.1 us -> 35.3 us (0.978)
  waiting for transfers between devices: 8.01 us -> 6.75 us
  Pallas kernels: 10.3 us -> 10.7 us
    ppermute x1, waiting for transfers between devices: 4.06 us -> 2.8 us  [body(): corner_down = lax.ppermute(corners_down, 'az', back)]
    pallas_call x0 -> x1, Pallas kernels: none -> 1.25 us  [body(): pl.pallas_call(fetch_kernel, in_specs=[away], out_shape=jax.ShapeDtypeStr...]
    pallas_call x1, Pallas kernels: 8.97 us -> 8.14 us  [body(): pl.pallas_call(functools.partial(main_kernel, pad, side), grid=(chip_rows...]
  transfers between devices with their start and end apart: 6 -> 6, of which waited for: 2 -> 2; matrix products, arithmetic and copies ran while one was open for 0% -> 0% of each run, Pallas kernels for 0% -> 4%
where the time goes in v4:
time: 35.3 us; the launch traced here: 35 us
  starting transfers between devices  17.4 us (49%)
  Pallas kernels  10.7 us (30%)
  waiting for transfers between devices  6.75 us (19%)
    pallas_call x1, Pallas kernels, body(): pl.pallas_call(functools.partial(main_kernel, pad, side), grid=(chip_rows...  8.14 us
    ppermute x1, starting transfers between devices, body(): left = lax.ppermute(to_right, 'rg', east)  4.24 us
    ppermute x1, starting transfers between devices, body(): corner_up = lax.ppermute(corners_up, 'az', forth)  4.05 us
    ppermute x1, waiting for transfers between devices, body(): right = lax.ppermute(to_left, 'rg', west)  3.94 us
    ppermute x1, starting transfers between devices, body(): up = lax.ppermute(to_up, 'az', forth)  3.15 us
    ppermute x1, waiting for transfers between devices, body(): corner_down = lax.ppermute(corners_down, 'az', back)  2.8 us
    ppermute x1, starting transfers between devices, body(): down = lax.ppermute(to_down, 'az', back)  2.13 us
    ppermute x1, starting transfers between devices, body(): right = lax.ppermute(to_left, 'rg', west)  1.92 us
  transfers between devices with their start and end apart: 6, of which 2 were waited for; matrix products, arithmetic and copies ran while one was open for 0% of the time, Pallas kernels for 4%

profile of v4, /device:TPU:21, one launch (start us, length us, event | category | flops | bytes accessed | tf_op | source)
XLA Modules:
  0.0 35.0 jit_solution(4322413317618260514)
XLA Ops:
  0.0 1.3 %shard_map.56 = (f32[128,768]{1,0:T(8,128)S(1)}, f32[128,768]{1,0:T(8,128)S(1)}, f32[104,768]{1,0:T(8,128)S(1)}, f32[104,768]{1,0:T(8,128)S(1)}, f32[128,128]{1,0:T(8,128)S(1)}, /*index=5*/f32[128,128]{1,0:T(8,128)S(1)}) custom-call(f32[128,768]{1,0:T(8,128)} %sec_hbm.1, f32[128,768]{1,0:T(8,128)} %ref_hbm.1), custom_call_target="tpu_custom_call" | custom-call | tf_op jit(solution)/shard_map/pallas_call | solution.py:332
  1.4 3.1 %collective-permute-start = (f32[104,768]{1,0:T(8,128)S(1)}, f32[104,768]{1,0:T(8,128)S(1)}, u32[]{:S(2)}, u32[]{:S(2)}) collective-permute-start(f32[104,768]{1,0:T(8,128)S(1)} %get-tuple-element.15), channel_id=1, source_target_pairs={{0,4},{4,8},{8,12},{12,16},{16,20},{20,24},{24,28},{1,5},{5,9},{9,... | collective-permute-start | bytes 958472 | tf_op jit(solution)/shard_map/ppermute | solution.py:341
  4.5 2.1 %collective-permute-start.1 = (f32[104,768]{1,0:T(8,128)S(1)}, f32[104,768]{1,0:T(8,128)S(1)}, u32[]{:S(2)}, u32[]{:S(2)}) collective-permute-start(f32[104,768]{1,0:T(8,128)S(1)} %get-tuple-element.16), channel_id=1, source_target_pairs={{4,0},{8,4},{12,8},{16,12},{20,16},{24,20},{28,24},{5,1},{9,5},{13... | collective-permute-start | bytes 958472 | tf_op jit(solution)/shard_map/ppermute | solution.py:342
  6.6 4.2 %collective-permute-start.2 = (f32[128,128]{1,0:T(8,128)S(1)}, f32[128,128]{1,0:T(8,128)S(1)}, u32[]{:S(2)}, u32[]{:S(2)}) collective-permute-start(f32[128,128]{1,0:T(8,128)S(1)} %get-tuple-element.17), channel_id=1, source_target_pairs={{0,1},{1,2},{2,3},{4,5},{5,6},{6,7},{8,9},{9,10},{10,11},{12,13},{... | collective-permute-start | bytes 196616 | tf_op jit(solution)/shard_map/ppermute | solution.py:343
  10.9 1.9 %collective-permute-start.3 = (f32[128,128]{1,0:T(8,128)S(1)}, f32[128,128]{1,0:T(8,128)S(1)}, u32[]{:S(2)}, u32[]{:S(2)}) collective-permute-start(f32[128,128]{1,0:T(8,128)S(1)} %get-tuple-element.18), channel_id=1, source_target_pairs={{1,0},{2,1},{3,2},{5,4},{6,5},{7,6},{9,8},{10,9},{11,10},{13,12},{... | collective-permute-start | bytes 196616 | tf_op jit(solution)/shard_map/ppermute | solution.py:344
  12.8 0.0 collective-permute-done.2.left
  12.8 3.9 %collective-permute-done.3.right = f32[128,128]{1,0:T(8,128)S(1)} collective-permute-done((f32[128,128]{1,0:T(8,128)S(1)}, f32[128,128]{1,0:T(8,128)S(1)}, u32[]{:S(2)}, u32[]{:S(2)}) %collective-permute-start.3) | collective-permute-done | bytes 65568 | tf_op jit(solution)/shard_map/ppermute | solution.py:344
  16.8 4.0 %collective-permute-start.4 = (f32[72,256]{1,0:T(8,128)S(1)}, f32[72,256]{1,0:T(8,128)S(1)}, u32[]{:S(2)}, u32[]{:S(2)}) collective-permute-start(f32[72,256]{1,0:T(8,128)S(1)} %get-tuple-element.19), channel_id=1, source_target_pairs={{0,4},{4,8},{8,12},{12,16},{16,20},{20,24},{24,28},{1,5},{5,9},{9,... | collective-permute-start | bytes 221192 | tf_op jit(solution)/shard_map/ppermute | solution.py:350
  20.8 1.9 %collective-permute-start.5 = (f32[72,256]{1,0:T(8,128)S(1)}, f32[72,256]{1,0:T(8,128)S(1)}, u32[]{:S(2)}, u32[]{:S(2)}) collective-permute-start(f32[72,256]{1,0:T(8,128)S(1)} %get-tuple-element.20), channel_id=1, source_target_pairs={{4,0},{8,4},{12,8},{16,12},{20,16},{24,20},{28,24},{5,1},{9,5},{13... | collective-permute-start | bytes 221192 | tf_op jit(solution)/shard_map/ppermute | solution.py:351
  22.8 1.3 %shard_map.55.slab = bf16[4288,128]{1,0:T(8,128)(2,1)S(1)} custom-call(bf16[4288,128]{1,0:T(8,128)(2,1)} %constant.2.clone.source), custom_call_target="tpu_custom_call" | custom-call | tf_op jit(solution)/shard_map/pallas_call | solution.py:354
  24.0 0.0 collective-permute-done.4.corner_up
  24.0 2.8 %collective-permute-done.5.corner_down = f32[72,256]{1,0:T(8,128)S(1)} collective-permute-done((f32[72,256]{1,0:T(8,128)S(1)}, f32[72,256]{1,0:T(8,128)S(1)}, u32[]{:S(2)}, u32[]{:S(2)}) %collective-permute-start.5) | collective-permute-done | bytes 73760 | tf_op jit(solution)/shard_map/ppermute | solution.py:351
  26.8 0.0 collective-permute-done.up
  26.8 0.0 collective-permute-done.1.down
  26.8 8.1 %shard_map.58 = f32[2,12,128,128]{3,2,1,0:T(8,128)} custom-call(s32[2]{0:T(128)} %off_az_hbm.1, s32[2]{0:T(128)} %off_rg_hbm.1, bf16[4288,128]{1,0:T(8,128)(2,1)S(1)} %shard_map.55.slab, f32[128,768]{1,0:T(8,128)S(1)} %get-tuple-element.13.sec, f32[128,768]{1,0:T(8,128)S(1)} %get-tuple-element.14.ref, f32[104,768]{1,0:T(8,128)S(1)} %collective-permute-done.up, ...), custom_call_target="tpu_custom_call" | custom-call | tf_op jit(solution)/shard_map/pallas_call | solution.py:367
  (1 shorter events, 0.0 us)
Async XLA Ops:
  1.4 25.5 %collective-permute-start = (f32[104,768]{1,0:T(8,128)S(1)}, f32[104,768]{1,0:T(8,128)S(1)}, u32[]{:S(2)}, u32[]{:S(2)}) collective-permute-start(f32[104,768]{1,0:T(8,128)S(1)} %get-tuple-element.15), channel_id=1, source_target_pairs={{0,4},{4,8},{8,12},{12,16},{16,20},{20,24},{24,28},{1,5},{5,9},{9,... | collective-permute-start | bytes 958472 | tf_op jit(solution)/shard_map/ppermute | solution.py:341
  4.5 22.3 %collective-permute-start.1 = (f32[104,768]{1,0:T(8,128)S(1)}, f32[104,768]{1,0:T(8,128)S(1)}, u32[]{:S(2)}, u32[]{:S(2)}) collective-permute-start(f32[104,768]{1,0:T(8,128)S(1)} %get-tuple-element.16), channel_id=1, source_target_pairs={{4,0},{8,4},{12,8},{16,12},{20,16},{24,20},{28,24},{5,1},{9,5},{13... | collective-permute-start | bytes 958472 | tf_op jit(solution)/shard_map/ppermute | solution.py:342
  6.6 6.2 %collective-permute-start.2 = (f32[128,128]{1,0:T(8,128)S(1)}, f32[128,128]{1,0:T(8,128)S(1)}, u32[]{:S(2)}, u32[]{:S(2)}) collective-permute-start(f32[128,128]{1,0:T(8,128)S(1)} %get-tuple-element.17), channel_id=1, source_target_pairs={{0,1},{1,2},{2,3},{4,5},{5,6},{6,7},{8,9},{9,10},{10,11},{12,13},{... | collective-permute-start | bytes 196616 | tf_op jit(solution)/shard_map/ppermute | solution.py:343
  10.9 5.9 %collective-permute-start.3 = (f32[128,128]{1,0:T(8,128)S(1)}, f32[128,128]{1,0:T(8,128)S(1)}, u32[]{:S(2)}, u32[]{:S(2)}) collective-permute-start(f32[128,128]{1,0:T(8,128)S(1)} %get-tuple-element.18), channel_id=1, source_target_pairs={{1,0},{2,1},{3,2},{5,4},{6,5},{7,6},{9,8},{10,9},{11,10},{13,12},{... | collective-permute-start | bytes 196616 | tf_op jit(solution)/shard_map/ppermute | solution.py:344
  16.8 7.2 %collective-permute-start.4 = (f32[72,256]{1,0:T(8,128)S(1)}, f32[72,256]{1,0:T(8,128)S(1)}, u32[]{:S(2)}, u32[]{:S(2)}) collective-permute-start(f32[72,256]{1,0:T(8,128)S(1)} %get-tuple-element.19), channel_id=1, source_target_pairs={{0,4},{4,8},{8,12},{12,16},{16,20},{20,24},{24,28},{1,5},{5,9},{9,... | collective-permute-start | bytes 221192 | tf_op jit(solution)/shard_map/ppermute | solution.py:350
  20.8 6.0 %collective-permute-start.5 = (f32[72,256]{1,0:T(8,128)S(1)}, f32[72,256]{1,0:T(8,128)S(1)}, u32[]{:S(2)}, u32[]{:S(2)}) collective-permute-start(f32[72,256]{1,0:T(8,128)S(1)} %get-tuple-element.20), channel_id=1, source_target_pairs={{4,0},{8,4},{12,8},{16,12},{20,16},{24,20},{28,24},{5,1},{9,5},{13... | collective-permute-start | bytes 221192 | tf_op jit(solution)/shard_map/ppermute | solution.py:351

commit v5 on v4

--- a/solution.py
+++ b/solution.py
@@ -122,12 +122,23 @@
         copy.wait()
 
 
-def corner_kernel(pad, left, right, up, down):
+def corner_kernel(pad, side, need, left, right, up, down):
     rows = left.shape[0]
-    up[:, :LANES] = left[rows - pad:]
-    up[:, LANES:] = right[rows - pad:]
-    down[:, :LANES] = left[:pad]
-    down[:, LANES:] = right[:pad]
+    half = up.shape[0] - pad
+    lane = lax.broadcasted_iota(jnp.int32, (1, LANES), 1)
+    spare = LANES - need
+
+    def tile(out, first, edge):
+        west, east = left[first:first + pad], right[first:first + pad]
+        out[0:pad] = jnp.where(lane < spare, east, west)
+        upper = pltpu.roll(east[:half], (side - spare) % LANES, 1)
+        lower = pltpu.roll(east[pad - half:], (2 * side - spare) % LANES, 1)
+        inner = jnp.where(lane < 2 * side, upper, lower)
+        inner = jnp.where(lane < side, west[edge:edge + half], inner)
+        out[pad:] = jnp.where(lane < 3 * side, inner, east[edge:edge + half])
+
+    tile(up, rows - pad, pad - half)
+    tile(down, 0, 0)
 
 
 def fetch_kernel(source, target, sem):
@@ -136,7 +147,7 @@
     copy.wait()
 
 
-def main_kernel(pad, side, off_az_hbm, off_rg_hbm, slab, sec, ref, up, down, left, right, corner_up,
+def main_kernel(pad, side, need, off_az_hbm, off_rg_hbm, slab, sec, ref, up, down, left, right, corner_up,
                 corner_down, out, off_az, off_rg, sec_ext, ref_ext, lhs, spec, zed, sems):
     rows, cols = sec.shape
     tiles = cols // LANES
@@ -161,16 +172,25 @@
         level_sec = jnp.sum(sec[...]) * (1.0 / (rows * cols))
         level_ref = jnp.sum(ref[...]) * (1.0 / (rows * cols))
         inner = slice(LANES, LANES + cols)
-        sec_ext[0:pad, 0:LANES] = corner_up[:, :LANES] - level_sec
+        lane = lax.broadcasted_iota(jnp.int32, (1, LANES), 1)
+        spare = LANES - need
+        half = corner_up.shape[0] - pad
+
+        def east_of(corner):
+            rest = corner[pad:]
+            upper = pltpu.roll(rest[:pad - half], (spare - side) % LANES, 1)
+            lower = pltpu.roll(rest, (spare - 2 * side) % LANES, 1)
+            return jnp.where(lane < spare, corner[0:pad], jnp.concatenate([upper, lower], axis=0))
+
+        sec_ext[0:pad, 0:LANES] = corner_up[0:pad] - level_sec
         sec_ext[0:pad, inner] = up[0:pad] - level_sec
-        sec_ext[0:pad, LANES + cols:] = corner_up[:, LANES:] - level_sec
+        sec_ext[0:pad, LANES + cols:] = east_of(corner_up) - level_sec
         sec_ext[pad:pad + rows, 0:LANES] = left[...] - level_sec
         sec_ext[pad:pad + rows, inner] = sec[...] - level_sec
         sec_ext[pad:pad + rows, LANES + cols:] = right[...] - level_sec
-        sec_ext[pad + rows:, 0:LANES] = corner_down[:, :LANES] - level_sec
+        sec_ext[pad + rows:, 0:LANES] = corner_down[0:pad] - level_sec
         sec_ext[pad + rows:, inner] = down[0:pad] - level_sec
-        sec_ext[pad + rows:, LANES + cols:] = corner_down[:, LANES:] - level_sec
-        lane = lax.broadcasted_iota(jnp.int32, (1, LANES), 1)
+        sec_ext[pad + rows:, LANES + cols:] = east_of(corner_down) - level_sec
 
         def place(at, west, middle, east):
             pieces = [pltpu.roll(west, LANES - side, 1)]
@@ -181,9 +201,9 @@
                 ref_ext[at:at + west.shape[0], t * LANES:(t + 1) * LANES] = jnp.where(
                     lane < side, turned[t], turned[t + 1]) - level_ref
 
-        place(0, corner_up[pad - side:, :LANES], up[pad:], corner_up[pad - side:, LANES:])
+        place(0, corner_up[pad + half - side:], up[pad:], corner_up[pad + half - side:])
         place(side, left[...], ref[...], right[...])
-        place(side + rows, corner_down[:side, :LANES], down[pad:], corner_down[:side, LANES:])
+        place(side + rows, corner_down[pad:pad + side], down[pad:], corner_down[pad:pad + side])
         for copy in copies:
             copy.wait()
 
@@ -320,7 +340,9 @@
     all_rows = chip_rows * lax.axis_size("az")
     reach = min(SPACE - 1, (all_rows - 1) // 2)
     pad = -(-(SPACE + reach) // 8) * 8
-    assert SPACE + reach + side <= LANES
+    need = SPACE + reach
+    half = -(-pad // 16) * 8
+    assert need + side <= LANES and half >= side and 2 * need - LANES <= side
     tiles = cols // LANES
 
     tall = rows + 2 * pad
@@ -343,8 +365,8 @@
     left = lax.ppermute(to_right, "rg", east)
     right = lax.ppermute(to_left, "rg", west)
     corners_up, corners_down = pl.pallas_call(
-        functools.partial(corner_kernel, pad),
-        out_shape=[full(pad, 2 * LANES)] * 2,
+        functools.partial(corner_kernel, pad, side, need),
+        out_shape=[full(pad + half, LANES)] * 2,
         compiler_params=pltpu.CompilerParams(vmem_limit_bytes=8 << 20),
     )(left, right)
     corner_up = lax.ppermute(corners_up, "az", forth)
@@ -365,7 +387,7 @@
         return pl.BlockSpec(x.shape, lambda i: (0, 0), pipeline_mode=pl.Buffered(1))
 
     return pl.pallas_call(
-        functools.partial(main_kernel, pad, side),
+        functools.partial(main_kernel, pad, side, need),
         grid=(chip_rows,),
         in_specs=[away] * 2 + [whole(x) for x in operands],
         out_specs=pl.BlockSpec((1, chip_cols, 2 * LAGS, 2 * LAGS), lambda i: (i, 0, 0, 0)),

time: 35.3 us -> 35.4 us (level)
  Pallas kernels: 10.7 us -> 11.1 us
where the time goes in v5:
time: 35.4 us; the launch traced here: 35.1 us
  starting transfers between devices  17.4 us (49%)
  Pallas kernels  11.1 us (31%)
  waiting for transfers between devices  6.57 us (19%)
    pallas_call x1, Pallas kernels, body(): pl.pallas_call(functools.partial(main_kernel, pad, side, need), grid=(chi...  8.39 us
    ppermute x1, starting transfers between devices, body(): left = lax.ppermute(to_right, 'rg', east)  4.24 us
    ppermute x1, starting transfers between devices, body(): corner_up = lax.ppermute(corners_up, 'az', forth)  4.05 us
    ppermute x1, waiting for transfers between devices, body(): right = lax.ppermute(to_left, 'rg', west)  3.94 us
    ppermute x1, starting transfers between devices, body(): up = lax.ppermute(to_up, 'az', forth)  3.15 us
    ppermute x1, waiting for transfers between devices, body(): corner_down = lax.ppermute(corners_down, 'az', back)  2.62 us
    ppermute x1, starting transfers between devices, body(): down = lax.ppermute(to_down, 'az', back)  2.13 us
    ppermute x1, starting transfers between devices, body(): right = lax.ppermute(to_left, 'rg', west)  1.92 us
  transfers between devices with their start and end apart: 6, of which 2 were waited for; matrix products, arithmetic and copies ran while one was open for 0% of the time, Pallas kernels for 4%

profile of v5, /device:TPU:21, one launch (start us, length us, event | category | flops | bytes accessed | tf_op | source)
XLA Modules:
  0.0 35.1 jit_solution(13441621971607585300)
XLA Ops:
  0.0 1.3 %shard_map.56 = (f32[128,768]{1,0:T(8,128)S(1)}, f32[128,768]{1,0:T(8,128)S(1)}, f32[104,768]{1,0:T(8,128)S(1)}, f32[104,768]{1,0:T(8,128)S(1)}, f32[128,128]{1,0:T(8,128)S(1)}, /*index=5*/f32[128,128]{1,0:T(8,128)S(1)}) custom-call(f32[128,768]{1,0:T(8,128)} %sec_hbm.1, f32[128,768]{1,0:T(8,128)} %ref_hbm.1), custom_call_target="tpu_custom_call" | custom-call | tf_op jit(solution)/shard_map/pallas_call | solution.py:354
  1.4 3.1 %collective-permute-start = (f32[104,768]{1,0:T(8,128)S(1)}, f32[104,768]{1,0:T(8,128)S(1)}, u32[]{:S(2)}, u32[]{:S(2)}) collective-permute-start(f32[104,768]{1,0:T(8,128)S(1)} %get-tuple-element.15), channel_id=1, source_target_pairs={{0,4},{4,8},{8,12},{12,16},{16,20},{20,24},{24,28},{1,5},{5,9},{9,... | collective-permute-start | bytes 958472 | tf_op jit(solution)/shard_map/ppermute | solution.py:363
  4.5 2.1 %collective-permute-start.1 = (f32[104,768]{1,0:T(8,128)S(1)}, f32[104,768]{1,0:T(8,128)S(1)}, u32[]{:S(2)}, u32[]{:S(2)}) collective-permute-start(f32[104,768]{1,0:T(8,128)S(1)} %get-tuple-element.16), channel_id=1, source_target_pairs={{4,0},{8,4},{12,8},{16,12},{20,16},{24,20},{28,24},{5,1},{9,5},{13... | collective-permute-start | bytes 958472 | tf_op jit(solution)/shard_map/ppermute | solution.py:364
  6.6 4.2 %collective-permute-start.2 = (f32[128,128]{1,0:T(8,128)S(1)}, f32[128,128]{1,0:T(8,128)S(1)}, u32[]{:S(2)}, u32[]{:S(2)}) collective-permute-start(f32[128,128]{1,0:T(8,128)S(1)} %get-tuple-element.17), channel_id=1, source_target_pairs={{0,1},{1,2},{2,3},{4,5},{5,6},{6,7},{8,9},{9,10},{10,11},{12,13},{... | collective-permute-start | bytes 196616 | tf_op jit(solution)/shard_map/ppermute | solution.py:365
  10.9 1.9 %collective-permute-start.3 = (f32[128,128]{1,0:T(8,128)S(1)}, f32[128,128]{1,0:T(8,128)S(1)}, u32[]{:S(2)}, u32[]{:S(2)}) collective-permute-start(f32[128,128]{1,0:T(8,128)S(1)} %get-tuple-element.18), channel_id=1, source_target_pairs={{1,0},{2,1},{3,2},{5,4},{6,5},{7,6},{9,8},{10,9},{11,10},{13,12},{... | collective-permute-start | bytes 196616 | tf_op jit(solution)/shard_map/ppermute | solution.py:366
  12.8 0.0 collective-permute-done.2.left
  12.8 3.9 %collective-permute-done.3.right = f32[128,128]{1,0:T(8,128)S(1)} collective-permute-done((f32[128,128]{1,0:T(8,128)S(1)}, f32[128,128]{1,0:T(8,128)S(1)}, u32[]{:S(2)}, u32[]{:S(2)}) %collective-permute-start.3) | collective-permute-done | bytes 65568 | tf_op jit(solution)/shard_map/ppermute | solution.py:366
  16.8 0.1 shard_map.57
  16.9 4.0 %collective-permute-start.4 = (f32[112,128]{1,0:T(8,128)S(1)}, f32[112,128]{1,0:T(8,128)S(1)}, u32[]{:S(2)}, u32[]{:S(2)}) collective-permute-start(f32[112,128]{1,0:T(8,128)S(1)} %get-tuple-element.19), channel_id=1, source_target_pairs={{0,4},{4,8},{8,12},{12,16},{16,20},{20,24},{24,28},{1,5},{5,9},{9,... | collective-permute-start | bytes 172040 | tf_op jit(solution)/shard_map/ppermute | solution.py:372
  20.9 1.9 %collective-permute-start.5 = (f32[112,128]{1,0:T(8,128)S(1)}, f32[112,128]{1,0:T(8,128)S(1)}, u32[]{:S(2)}, u32[]{:S(2)}) collective-permute-start(f32[112,128]{1,0:T(8,128)S(1)} %get-tuple-element.20), channel_id=1, source_target_pairs={{4,0},{8,4},{12,8},{16,12},{20,16},{24,20},{28,24},{5,1},{9,5},{13... | collective-permute-start | bytes 172040 | tf_op jit(solution)/shard_map/ppermute | solution.py:373
  22.9 1.3 %shard_map.55.slab = bf16[4288,128]{1,0:T(8,128)(2,1)S(1)} custom-call(bf16[4288,128]{1,0:T(8,128)(2,1)} %constant.2.clone.source), custom_call_target="tpu_custom_call" | custom-call | tf_op jit(solution)/shard_map/pallas_call | solution.py:376
  24.1 0.0 collective-permute-done.4.corner_up
  24.1 2.6 %collective-permute-done.5.corner_down = f32[112,128]{1,0:T(8,128)S(1)} collective-permute-done((f32[112,128]{1,0:T(8,128)S(1)}, f32[112,128]{1,0:T(8,128)S(1)}, u32[]{:S(2)}, u32[]{:S(2)}) %collective-permute-start.5) | collective-permute-done | bytes 57376 | tf_op jit(solution)/shard_map/ppermute | solution.py:373
  26.7 0.0 collective-permute-done.up
  26.8 0.0 collective-permute-done.1.down
  26.8 8.4 %shard_map.58 = f32[2,12,128,128]{3,2,1,0:T(8,128)} custom-call(s32[2]{0:T(128)} %off_az_hbm.1, s32[2]{0:T(128)} %off_rg_hbm.1, bf16[4288,128]{1,0:T(8,128)(2,1)S(1)} %shard_map.55.slab, f32[128,768]{1,0:T(8,128)S(1)} %get-tuple-element.13.sec, f32[128,768]{1,0:T(8,128)S(1)} %get-tuple-element.14.ref, f32[104,768]{1,0:T(8,128)S(1)} %collective-permute-done.up, ...), custom_call_target="tpu_custom_call" | custom-call | tf_op jit(solution)/shard_map/pallas_call | solution.py:389
Async XLA Ops:
  1.4 25.4 %collective-permute-start = (f32[104,768]{1,0:T(8,128)S(1)}, f32[104,768]{1,0:T(8,128)S(1)}, u32[]{:S(2)}, u32[]{:S(2)}) collective-permute-start(f32[104,768]{1,0:T(8,128)S(1)} %get-tuple-element.15), channel_id=1, source_target_pairs={{0,4},{4,8},{8,12},{12,16},{16,20},{20,24},{24,28},{1,5},{5,9},{9,... | collective-permute-start | bytes 958472 | tf_op jit(solution)/shard_map/ppermute | solution.py:363
  4.5 22.2 %collective-permute-start.1 = (f32[104,768]{1,0:T(8,128)S(1)}, f32[104,768]{1,0:T(8,128)S(1)}, u32[]{:S(2)}, u32[]{:S(2)}) collective-permute-start(f32[104,768]{1,0:T(8,128)S(1)} %get-tuple-element.16), channel_id=1, source_target_pairs={{4,0},{8,4},{12,8},{16,12},{20,16},{24,20},{28,24},{5,1},{9,5},{13... | collective-permute-start | bytes 958472 | tf_op jit(solution)/shard_map/ppermute | solution.py:364
  6.6 6.2 %collective-permute-start.2 = (f32[128,128]{1,0:T(8,128)S(1)}, f32[128,128]{1,0:T(8,128)S(1)}, u32[]{:S(2)}, u32[]{:S(2)}) collective-permute-start(f32[128,128]{1,0:T(8,128)S(1)} %get-tuple-element.17), channel_id=1, source_target_pairs={{0,1},{1,2},{2,3},{4,5},{5,6},{6,7},{8,9},{9,10},{10,11},{12,13},{... | collective-permute-start | bytes 196616 | tf_op jit(solution)/shard_map/ppermute | solution.py:365
  10.9 5.9 %collective-permute-start.3 = (f32[128,128]{1,0:T(8,128)S(1)}, f32[128,128]{1,0:T(8,128)S(1)}, u32[]{:S(2)}, u32[]{:S(2)}) collective-permute-start(f32[128,128]{1,0:T(8,128)S(1)} %get-tuple-element.18), channel_id=1, source_target_pairs={{1,0},{2,1},{3,2},{5,4},{6,5},{7,6},{9,8},{10,9},{11,10},{13,12},{... | collective-permute-start | bytes 196616 | tf_op jit(solution)/shard_map/ppermute | solution.py:366
  16.9 7.2 %collective-permute-start.4 = (f32[112,128]{1,0:T(8,128)S(1)}, f32[112,128]{1,0:T(8,128)S(1)}, u32[]{:S(2)}, u32[]{:S(2)}) collective-permute-start(f32[112,128]{1,0:T(8,128)S(1)} %get-tuple-element.19), channel_id=1, source_target_pairs={{0,4},{4,8},{8,12},{12,16},{16,20},{20,24},{24,28},{1,5},{5,9},{9,... | collective-permute-start | bytes 172040 | tf_op jit(solution)/shard_map/ppermute | solution.py:372
  20.9 5.8 %collective-permute-start.5 = (f32[112,128]{1,0:T(8,128)S(1)}, f32[112,128]{1,0:T(8,128)S(1)}, u32[]{:S(2)}, u32[]{:S(2)}) collective-permute-start(f32[112,128]{1,0:T(8,128)S(1)} %get-tuple-element.20), channel_id=1, source_target_pairs={{4,0},{8,4},{12,8},{16,12},{20,16},{24,20},{28,24},{5,1},{9,5},{13... | collective-permute-start | bytes 172040 | tf_op jit(solution)/shard_map/ppermute | solution.py:373

commit v6 on v5

--- a/solution.py
+++ b/solution.py
@@ -141,13 +141,16 @@
     tile(down, 0, 0)
 
 
-def fetch_kernel(source, target, sem):
+def fetch_kernel(source, sec, ref, target, levels, sem):
     copy = pltpu.make_async_copy(source, target, sem)
     copy.start()
+    scale = 1.0 / (sec.shape[0] * sec.shape[1])
+    levels[0:8] = jnp.full((8, LANES), jnp.sum(sec[...]) * scale, F32)
+    levels[8:16] = jnp.full((8, LANES), jnp.sum(ref[...]) * scale, F32)
     copy.wait()
 
 
-def main_kernel(pad, side, need, off_az_hbm, off_rg_hbm, slab, sec, ref, up, down, left, right, corner_up,
+def main_kernel(pad, side, need, off_az_hbm, off_rg_hbm, slab, levels, sec, ref, up, down, left, right, corner_up,
                 corner_down, out, off_az, off_rg, sec_ext, ref_ext, lhs, spec, zed, sems):
     rows, cols = sec.shape
     tiles = cols // LANES
@@ -169,8 +172,8 @@
         ]
         for copy in copies:
             copy.start()
-        level_sec = jnp.sum(sec[...]) * (1.0 / (rows * cols))
-        level_ref = jnp.sum(ref[...]) * (1.0 / (rows * cols))
+        level_sec, level_ref = levels[0:1], levels[8:9]
+        level_wide = jnp.concatenate([level_sec] * tiles, axis=1)
         inner = slice(LANES, LANES + cols)
         lane = lax.broadcasted_iota(jnp.int32, (1, LANES), 1)
         spare = LANES - need
@@ -183,13 +186,13 @@
             return jnp.where(lane < spare, corner[0:pad], jnp.concatenate([upper, lower], axis=0))
 
         sec_ext[0:pad, 0:LANES] = corner_up[0:pad] - level_sec
-        sec_ext[0:pad, inner] = up[0:pad] - level_sec
+        sec_ext[0:pad, inner] = up[0:pad] - level_wide
         sec_ext[0:pad, LANES + cols:] = east_of(corner_up) - level_sec
         sec_ext[pad:pad + rows, 0:LANES] = left[...] - level_sec
-        sec_ext[pad:pad + rows, inner] = sec[...] - level_sec
+        sec_ext[pad:pad + rows, inner] = sec[...] - level_wide
         sec_ext[pad:pad + rows, LANES + cols:] = right[...] - level_sec
         sec_ext[pad + rows:, 0:LANES] = corner_down[0:pad] - level_sec
-        sec_ext[pad + rows:, inner] = down[0:pad] - level_sec
+        sec_ext[pad + rows:, inner] = down[0:pad] - level_wide
         sec_ext[pad + rows:, LANES + cols:] = east_of(corner_down) - level_sec
 
         def place(at, west, middle, east):
@@ -373,14 +376,14 @@
     corner_down = lax.ppermute(corners_down, "az", back)
 
     slab = jnp.asarray(tables()[0])
-    held = pl.pallas_call(
+    held, levels = pl.pallas_call(
         fetch_kernel,
-        in_specs=[away],
-        out_shape=jax.ShapeDtypeStruct(slab.shape, BF16),
+        in_specs=[away] + [pl.BlockSpec(memory_space=pltpu.MemorySpace.VMEM)] * 2,
+        out_shape=[jax.ShapeDtypeStruct(slab.shape, BF16), full(16, LANES)],
         scratch_shapes=[pltpu.SemaphoreType.DMA],
         compiler_params=pltpu.CompilerParams(vmem_limit_bytes=8 << 20),
-    )(pltpu.with_memory_space_constraint(slab, pltpu.MemorySpace.HBM))
-    operands = [held, sec, ref, up, down, left, right, corner_up, corner_down]
+    )(pltpu.with_memory_space_constraint(slab, pltpu.MemorySpace.HBM), sec, ref)
+    operands = [held, levels, sec, ref, up, down, left, right, corner_up, corner_down]
     count = tiles + 1
 
     def whole(x):

time: 35.4 us -> 35.6 us (level)
  no operation moved by 1% of the time
where the time goes in v6:
time: 35.6 us; the launch traced here: 35.3 us
  starting transfers between devices  17.4 us (49%)
  Pallas kernels  11.2 us (31%)
  waiting for transfers between devices  6.57 us (18%)
    pallas_call x1, Pallas kernels, body(): pl.pallas_call(functools.partial(main_kernel, pad, side, need), grid=(chi...  8.51 us
    ppermute x1, starting transfers between devices, body(): left = lax.ppermute(to_right, 'rg', east)  4.24 us
    ppermute x1, starting transfers between devices, body(): corner_up = lax.ppermute(corners_up, 'az', forth)  4.05 us
    ppermute x1, waiting for transfers between devices, body(): right = lax.ppermute(to_left, 'rg', west)  3.94 us
    ppermute x1, starting transfers between devices, body(): up = lax.ppermute(to_up, 'az', forth)  3.15 us
    ppermute x1, waiting for transfers between devices, body(): corner_down = lax.ppermute(corners_down, 'az', back)  2.62 us
    ppermute x1, starting transfers between devices, body(): down = lax.ppermute(to_down, 'az', back)  2.13 us
    ppermute x1, starting transfers between devices, body(): right = lax.ppermute(to_left, 'rg', west)  1.92 us
  transfers between devices with their start and end apart: 6, of which 2 were waited for; matrix products, arithmetic and copies ran while one was open for 0% of the time, Pallas kernels for 4%

profile of v6, /device:TPU:21, one launch (start us, length us, event | category | flops | bytes accessed | tf_op | source)
XLA Modules:
  0.0 35.3 jit_solution(1167768615895862003)
XLA Ops:
  0.0 1.3 %shard_map.55 = (f32[128,768]{1,0:T(8,128)S(1)}, f32[128,768]{1,0:T(8,128)S(1)}, f32[104,768]{1,0:T(8,128)S(1)}, f32[104,768]{1,0:T(8,128)S(1)}, f32[128,128]{1,0:T(8,128)S(1)}, /*index=5*/f32[128,128]{1,0:T(8,128)S(1)}) custom-call(f32[128,768]{1,0:T(8,128)} %sec_hbm.1, f32[128,768]{1,0:T(8,128)} %ref_hbm.1), custom_call_target="tpu_custom_call" | custom-call | tf_op jit(solution)/shard_map/pallas_call | solution.py:357
  1.4 3.1 %collective-permute-start = (f32[104,768]{1,0:T(8,128)S(1)}, f32[104,768]{1,0:T(8,128)S(1)}, u32[]{:S(2)}, u32[]{:S(2)}) collective-permute-start(f32[104,768]{1,0:T(8,128)S(1)} %get-tuple-element.19), channel_id=1, source_target_pairs={{0,4},{4,8},{8,12},{12,16},{16,20},{20,24},{24,28},{1,5},{5,9},{9,... | collective-permute-start | bytes 958472 | tf_op jit(solution)/shard_map/ppermute | solution.py:366
  4.5 2.1 %collective-permute-start.1 = (f32[104,768]{1,0:T(8,128)S(1)}, f32[104,768]{1,0:T(8,128)S(1)}, u32[]{:S(2)}, u32[]{:S(2)}) collective-permute-start(f32[104,768]{1,0:T(8,128)S(1)} %get-tuple-element.20), channel_id=1, source_target_pairs={{4,0},{8,4},{12,8},{16,12},{20,16},{24,20},{28,24},{5,1},{9,5},{13... | collective-permute-start | bytes 958472 | tf_op jit(solution)/shard_map/ppermute | solution.py:367
  6.6 4.2 %collective-permute-start.2 = (f32[128,128]{1,0:T(8,128)S(1)}, f32[128,128]{1,0:T(8,128)S(1)}, u32[]{:S(2)}, u32[]{:S(2)}) collective-permute-start(f32[128,128]{1,0:T(8,128)S(1)} %get-tuple-element.21), channel_id=1, source_target_pairs={{0,1},{1,2},{2,3},{4,5},{5,6},{6,7},{8,9},{9,10},{10,11},{12,13},{... | collective-permute-start | bytes 196616 | tf_op jit(solution)/shard_map/ppermute | solution.py:368
  10.9 1.9 %collective-permute-start.3 = (f32[128,128]{1,0:T(8,128)S(1)}, f32[128,128]{1,0:T(8,128)S(1)}, u32[]{:S(2)}, u32[]{:S(2)}) collective-permute-start(f32[128,128]{1,0:T(8,128)S(1)} %get-tuple-element.22), channel_id=1, source_target_pairs={{1,0},{2,1},{3,2},{5,4},{6,5},{7,6},{9,8},{10,9},{11,10},{13,12},{... | collective-permute-start | bytes 196616 | tf_op jit(solution)/shard_map/ppermute | solution.py:369
  12.8 0.0 collective-permute-done.2.left
  12.8 3.9 %collective-permute-done.3.right = f32[128,128]{1,0:T(8,128)S(1)} collective-permute-done((f32[128,128]{1,0:T(8,128)S(1)}, f32[128,128]{1,0:T(8,128)S(1)}, u32[]{:S(2)}, u32[]{:S(2)}) %collective-permute-start.3) | collective-permute-done | bytes 65568 | tf_op jit(solution)/shard_map/ppermute | solution.py:369
  16.8 0.1 shard_map.57
  16.9 4.0 %collective-permute-start.4 = (f32[112,128]{1,0:T(8,128)S(1)}, f32[112,128]{1,0:T(8,128)S(1)}, u32[]{:S(2)}, u32[]{:S(2)}) collective-permute-start(f32[112,128]{1,0:T(8,128)S(1)} %get-tuple-element.23), channel_id=1, source_target_pairs={{0,4},{4,8},{8,12},{12,16},{16,20},{20,24},{24,28},{1,5},{5,9},{9,... | collective-permute-start | bytes 172040 | tf_op jit(solution)/shard_map/ppermute | solution.py:375
  20.9 1.9 %collective-permute-start.5 = (f32[112,128]{1,0:T(8,128)S(1)}, f32[112,128]{1,0:T(8,128)S(1)}, u32[]{:S(2)}, u32[]{:S(2)}) collective-permute-start(f32[112,128]{1,0:T(8,128)S(1)} %get-tuple-element.24), channel_id=1, source_target_pairs={{4,0},{8,4},{12,8},{16,12},{20,16},{24,20},{28,24},{5,1},{9,5},{13... | collective-permute-start | bytes 172040 | tf_op jit(solution)/shard_map/ppermute | solution.py:376
  22.9 1.3 %shard_map.56 = (bf16[4288,128]{1,0:T(8,128)(2,1)S(1)}, f32[16,128]{1,0:T(8,128)S(1)}) custom-call(bf16[4288,128]{1,0:T(8,128)(2,1)} %constant.2.clone.source, f32[128,768]{1,0:T(8,128)S(1)} %get-tuple-element.15.sec, f32[128,768]{1,0:T(8,128)S(1)} %get-tuple-element.16.ref), custom_call_target="tpu_custom_call" | custom-call | tf_op jit(solution)/shard_map/pallas_call | solution.py:379
  24.1 0.0 collective-permute-done.4.corner_up
  24.1 2.6 %collective-permute-done.5.corner_down = f32[112,128]{1,0:T(8,128)S(1)} collective-permute-done((f32[112,128]{1,0:T(8,128)S(1)}, f32[112,128]{1,0:T(8,128)S(1)}, u32[]{:S(2)}, u32[]{:S(2)}) %collective-permute-start.5) | collective-permute-done | bytes 57376 | tf_op jit(solution)/shard_map/ppermute | solution.py:376
  26.7 0.0 collective-permute-done.up
  26.7 0.0 collective-permute-done.1.down
  26.8 8.5 %shard_map.58 = f32[2,12,128,128]{3,2,1,0:T(8,128)} custom-call(s32[2]{0:T(128)} %off_az_hbm.1, s32[2]{0:T(128)} %off_rg_hbm.1, bf16[4288,128]{1,0:T(8,128)(2,1)S(1)} %get-tuple-element.17.slab, f32[16,128]{1,0:T(8,128)S(1)} %get-tuple-element.18.levels, f32[128,768]{1,0:T(8,128)S(1)} %get-tuple-element.15.sec, f32[128,768]{1,0:T(8,128)S(1)} %get-tuple-element.16.ref, ...), custom_call_target="tpu_custom_call" | custom-call | tf_op jit(solution)/shard_map/pallas_call | solution.py:392
Async XLA Ops:
  1.4 25.4 %collective-permute-start = (f32[104,768]{1,0:T(8,128)S(1)}, f32[104,768]{1,0:T(8,128)S(1)}, u32[]{:S(2)}, u32[]{:S(2)}) collective-permute-start(f32[104,768]{1,0:T(8,128)S(1)} %get-tuple-element.19), channel_id=1, source_target_pairs={{0,4},{4,8},{8,12},{12,16},{16,20},{20,24},{24,28},{1,5},{5,9},{9,... | collective-permute-start | bytes 958472 | tf_op jit(solution)/shard_map/ppermute | solution.py:366
  4.5 22.2 %collective-permute-start.1 = (f32[104,768]{1,0:T(8,128)S(1)}, f32[104,768]{1,0:T(8,128)S(1)}, u32[]{:S(2)}, u32[]{:S(2)}) collective-permute-start(f32[104,768]{1,0:T(8,128)S(1)} %get-tuple-element.20), channel_id=1, source_target_pairs={{4,0},{8,4},{12,8},{16,12},{20,16},{24,20},{28,24},{5,1},{9,5},{13... | collective-permute-start | bytes 958472 | tf_op jit(solution)/shard_map/ppermute | solution.py:367
  6.6 6.2 %collective-permute-start.2 = (f32[128,128]{1,0:T(8,128)S(1)}, f32[128,128]{1,0:T(8,128)S(1)}, u32[]{:S(2)}, u32[]{:S(2)}) collective-permute-start(f32[128,128]{1,0:T(8,128)S(1)} %get-tuple-element.21), channel_id=1, source_target_pairs={{0,1},{1,2},{2,3},{4,5},{5,6},{6,7},{8,9},{9,10},{10,11},{12,13},{... | collective-permute-start | bytes 196616 | tf_op jit(solution)/shard_map/ppermute | solution.py:368
  10.9 5.9 %collective-permute-start.3 = (f32[128,128]{1,0:T(8,128)S(1)}, f32[128,128]{1,0:T(8,128)S(1)}, u32[]{:S(2)}, u32[]{:S(2)}) collective-permute-start(f32[128,128]{1,0:T(8,128)S(1)} %get-tuple-element.22), channel_id=1, source_target_pairs={{1,0},{2,1},{3,2},{5,4},{6,5},{7,6},{9,8},{10,9},{11,10},{13,12},{... | collective-permute-start | bytes 196616 | tf_op jit(solution)/shard_map/ppermute | solution.py:369
  16.9 7.2 %collective-permute-start.4 = (f32[112,128]{1,0:T(8,128)S(1)}, f32[112,128]{1,0:T(8,128)S(1)}, u32[]{:S(2)}, u32[]{:S(2)}) collective-permute-start(f32[112,128]{1,0:T(8,128)S(1)} %get-tuple-element.23), channel_id=1, source_target_pairs={{0,4},{4,8},{8,12},{12,16},{16,20},{20,24},{24,28},{1,5},{5,9},{9,... | collective-permute-start | bytes 172040 | tf_op jit(solution)/shard_map/ppermute | solution.py:375
  20.9 5.8 %collective-permute-start.5 = (f32[112,128]{1,0:T(8,128)S(1)}, f32[112,128]{1,0:T(8,128)S(1)}, u32[]{:S(2)}, u32[]{:S(2)}) collective-permute-start(f32[112,128]{1,0:T(8,128)S(1)} %get-tuple-element.24), channel_id=1, source_target_pairs={{4,0},{8,4},{12,8},{16,12},{20,16},{24,20},{28,24},{5,1},{9,5},{13... | collective-permute-start | bytes 172040 | tf_op jit(solution)/shard_map/ppermute | solution.py:376
